TPU v7x, 8 devices: a whole 2x2x1 slice. The times are simulated.
8 devices in a mesh: dp: 2 (over z, y), kv: 4 (over x, core).
Axes of the slice: x: 2, y: 2, z: 1, core: 2. Of those that a mesh axis runs over, the one named last changes fastest.
Arguments:
- x_first: bfloat16 [32, 1024], P('dp'), parts along dimension 0
- next_emb: bfloat16 [2, 32, 1024], P(None, 'dp'), parts along dimension 1
- k_cache: bfloat16 [32, 1024, 8, 64], P('dp', 'kv'), parts along dimension 0
- v_cache: bfloat16 [32, 1024, 8, 64], P('dp', 'kv'), parts along dimension 0
- seq_len: int32 [32], P('dp'), parts along dimension 0
- ln1_gain: float32 [1024], replicated
- ln1_bias: float32 [1024], replicated
- w_q: bfloat16 [1024, 1024], replicated
- b_q: float32 [1024], replicated
- w_k: bfloat16 [1024, 512], replicated
- b_k: float32 [512], replicated
- w_v: bfloat16 [1024, 512], replicated
- b_v: float32 [512], replicated
- w_o: bfloat16 [1024, 1024], replicated
- b_o: float32 [1024], replicated
- ln2_gain: float32 [1024], replicated
- ln2_bias: float32 [1024], replicated
- w_router: bfloat16 [1024, 32], replicated
- w_gate: bfloat16 [32, 1024, 512], P(None, None, 'kv')
- w_up: bfloat16 [32, 1024, 512], P(None, None, 'kv')
- w_down: bfloat16 [32, 512, 1024], P(None, 'kv')
- long_factor: float32 [32], replicated
- expert_idx: int32 [3, 32, 8], P(None, 'dp'), parts along dimension 1
- route_mask: int32 [3, 32, 8, 32], P(None, 'dp'), parts along dimension 1
Outputs:
- output 1: bfloat16 [3, 32, 1024], P(None, 'dp'), parts along dimension 1
- output 2: bfloat16 [32, 3, 8, 64], P('dp'), parts along dimension 0
- output 3: bfloat16 [32, 3, 8, 64], P('dp'), parts along dimension 0
There are 2 independent parts. A program takes and returns all parts, laid end to end along the dimension named above; an argument that names none is the same for every part.
All inputs are finite; a program needn't handle non-finite values.
Results may differ from a plain program's by a relative error of at most 0.0125824.
Values sent between devices are 32-bit elements.
A program may use at most 1 GiB of HBM per device.

v0:
```python
import math
import jax
import jax.numpy as jnp
from jax import lax
from jax.sharding import PartitionSpec as P

ROPE_BASE = 10000.0
ROPE_MSCALE = math.sqrt(1.0 + math.log(32.0) / math.log(4096.0))
NORM_EPS = 1e-5
NEG_FILL = -1e30


def layer_norm(x_in, gain_vec, bias_vec):
    x_f32 = x_in.astype(jnp.float32)
    mean_val = jnp.mean(x_f32, axis=-1, keepdims=True)
    centered = x_f32 - mean_val
    var_val = jnp.mean(centered * centered, axis=-1, keepdims=True)
    return (centered * lax.rsqrt(var_val + NORM_EPS) * gain_vec + bias_vec).astype(jnp.bfloat16)


def rotate_heads(x_in, angles):
    half_dim = x_in.shape[-1] // 2
    cos_half = jnp.cos(angles) * ROPE_MSCALE
    sin_half = jnp.sin(angles) * ROPE_MSCALE
    cos_full = jnp.concatenate([cos_half, cos_half], axis=-1)[:, None, :]
    sin_full = jnp.concatenate([sin_half, sin_half], axis=-1)[:, None, :]
    x_f32 = x_in.astype(jnp.float32)
    rotated = jnp.concatenate([-x_f32[..., half_dim:], x_f32[..., :half_dim]], axis=-1)
    return (x_f32 * cos_full + rotated * sin_full).astype(jnp.bfloat16)


def inverse_freq(long_factor, head_dim):
    half_dim = head_dim // 2
    return 1.0 / (long_factor * ROPE_BASE ** (jnp.arange(half_dim, dtype=jnp.float32) * 2.0 / head_dim))


def partial_stats(q_grp, keys, values, keep_mask):
    scores = jnp.einsum('bkgd,btkd->bkgt', q_grp, keys, preferred_element_type=jnp.float32) * (q_grp.shape[-1] ** -0.5)
    keep_full = keep_mask[:, None, None, :]
    scores = jnp.where(keep_full, scores, NEG_FILL)
    run_max = jnp.max(scores, axis=-1)
    weights = jnp.where(keep_full, jnp.exp(scores - run_max[..., None]), 0.0)
    run_sum = jnp.sum(weights, axis=-1)
    out_part = jnp.einsum('bkgt,btkd->bkgd', weights.astype(jnp.bfloat16), values, preferred_element_type=jnp.float32)
    return run_max, run_sum, out_part


def combine_stats(max_all, sum_all, out_all):
    top_max = jnp.max(max_all, axis=0, keepdims=True)
    factor = jnp.exp(max_all - top_max)
    total_sum = jnp.sum(sum_all * factor, axis=0)
    merged = jnp.sum(out_all * factor[..., None], axis=0)
    return merged / total_sum[..., None]


def gate_matrix(h_moe, w_router, idx_step, mask_step):
    logits = jnp.dot(h_moe, w_router, preferred_element_type=jnp.float32)
    masked = jnp.where(mask_step == 1, logits[:, None, :], NEG_FILL)
    gate_probs = jax.nn.softmax(masked, axis=-1)
    chosen = idx_step[..., None] == jnp.arange(logits.shape[-1])[None, None, :]
    return jnp.sum(jnp.where(chosen, gate_probs, 0.0), axis=1)


def expert_part(h_moe, gate_mat, w_gate, w_up, w_down):
    act_gate = jnp.einsum('bd,edf->bef', h_moe, w_gate, preferred_element_type=jnp.float32)
    act_up = jnp.einsum('bd,edf->bef', h_moe, w_up, preferred_element_type=jnp.float32)
    mixed_act = (gate_mat[:, :, None] * jax.nn.silu(act_gate) * act_up).astype(jnp.bfloat16)
    return jnp.einsum('bef,efd->bd', mixed_act, w_down, preferred_element_type=jnp.float32).astype(jnp.bfloat16)


def solution(mesh):
    def layer_steps(x_first, next_emb, k_cache, v_cache, seq_len, ln1_gain, ln1_bias, w_q, b_q, w_k, b_k, w_v, b_v, w_o, b_o, ln2_gain, ln2_bias, w_router, w_gate, w_up, w_down, long_factor, expert_idx, route_mask):
        batch_rows, shard_len, kv_heads, head_dim = k_cache.shape
        q_heads = w_q.shape[1] // head_dim
        q_group = q_heads // kv_heads
        shard_id = lax.axis_index('kv')
        positions = shard_id * shard_len + jnp.arange(shard_len)
        cache_keep = positions[None, :] < seq_len[:, None]
        inv_freq = inverse_freq(long_factor, head_dim)
        step_inputs = [x_first] + [next_emb[emb_idx] for emb_idx in range(next_emb.shape[0])]
        new_keys = []
        new_values = []
        hidden = []
        for step_idx, x_in in enumerate(step_inputs):
            h_norm = layer_norm(x_in, ln1_gain, ln1_bias)
            q_new = (jnp.dot(h_norm, w_q, preferred_element_type=jnp.float32) + b_q).astype(jnp.bfloat16).reshape(batch_rows, q_heads, head_dim)
            k_new = (jnp.dot(h_norm, w_k, preferred_element_type=jnp.float32) + b_k).astype(jnp.bfloat16).reshape(batch_rows, kv_heads, head_dim)
            v_new = (jnp.dot(h_norm, w_v, preferred_element_type=jnp.float32) + b_v).astype(jnp.bfloat16).reshape(batch_rows, kv_heads, head_dim)
            angles = (seq_len + step_idx).astype(jnp.float32)[:, None] * inv_freq[None, :]
            q_grp = rotate_heads(q_new, angles).reshape(batch_rows, kv_heads, q_group, head_dim)
            new_keys.append(rotate_heads(k_new, angles))
            new_values.append(v_new)
            tail_k = jnp.stack(new_keys, axis=1)
            tail_v = jnp.stack(new_values, axis=1)
            run_max, run_sum, out_part = partial_stats(q_grp, k_cache, v_cache, cache_keep)
            packed = jnp.concatenate([run_max[..., None], run_sum[..., None], out_part], axis=-1)
            gathered = lax.all_gather(packed, 'kv')
            tail_keep = jnp.ones((batch_rows, step_idx + 1), jnp.bool_)
            tail_max, tail_sum, tail_out = partial_stats(q_grp, tail_k, tail_v, tail_keep)
            max_all = jnp.concatenate([gathered[..., 0], tail_max[None]], axis=0)
            sum_all = jnp.concatenate([gathered[..., 1], tail_sum[None]], axis=0)
            out_all = jnp.concatenate([gathered[..., 2:], tail_out[None]], axis=0)
            attn_out = combine_stats(max_all, sum_all, out_all).reshape(batch_rows, q_heads * head_dim).astype(jnp.bfloat16)
            x_mid = (x_in.astype(jnp.float32) + jnp.dot(attn_out, w_o, preferred_element_type=jnp.float32) + b_o).astype(jnp.bfloat16)
            h_moe = layer_norm(x_mid, ln2_gain, ln2_bias)
            gate_mat = gate_matrix(h_moe, w_router, expert_idx[step_idx], route_mask[step_idx])
            moe_part = expert_part(h_moe, gate_mat, w_gate, w_up, w_down)
            moe_sum = lax.psum(moe_part.astype(jnp.float32), 'kv')
            hidden.append((x_mid.astype(jnp.float32) + moe_sum).astype(jnp.bfloat16))
        return jnp.stack(hidden, axis=0), tail_k, tail_v

    replicated = P()
    in_specs = (P('dp'), P(None, 'dp'), P('dp', 'kv'), P('dp', 'kv'), P('dp')) + (replicated,) * 13 + (P(None, None, 'kv'), P(None, None, 'kv'), P(None, 'kv'), replicated, P(None, 'dp'), P(None, 'dp'))
    out_specs = (P(None, 'dp'), P('dp'), P('dp'))
    return jax.shard_map(layer_steps, mesh=mesh, in_specs=in_specs, out_specs=out_specs, check_vma=False)
```

profile of v0, /device:TPU:0, one launch (start us, length us, event | category | flops | bytes accessed | tf_op | source)
XLA Modules:
  0.0 227.0 jit_solution(14183510373880431406)
XLA Ops:
  9.4 2.0 fusion.34
  12.9 2.0 fusion.40
  16.2 2.7 %fusion.28 = f32[16,1024]{1,0:T(8,128)} fusion(bf16[1024,1024]{1,0:T(8,128)(2,1)} %param.31, f32[1024]{0:T(1024)S(1)} %copy-done.40, bf16[16,1024]{1,0:T(8,128)(2,1)S(1)} %copy-done.6, f32[1024]{0:T(1024)S(1)} %copy-done.25, f32[1024]{0:T(1024)S(1)} %copy-done.26, f32[16]{0:T(128)S(1)} %add_rsqrt_fusion.5, f32[16]{0:T(128)S(1)} %broadcast_multiply_fusion.5), kind=kOutput, calls=%fused_computation.47 | convolution fusion | flops 33701888 | bytes 2207872 | tf_op jit(solution)/shard_map/dot_general | solution.py:86
  19.8 1.6 reshape.459
  33.4 3.0 %fusion.229 = (f32[16,8,2]{2,1,0:T(8,128)S(1)}, f32[16,8,2,256]{3,2,1,0:T(2,128)S(1)}) fusion(bf16[16,8,2,64]{3,2,1,0:T(2,128)(2,1)S(1)} %fusion.78, bf16[16,256,8,64]{1,3,2,0:T(8,128)(2,1)} %param.26, pred[16,256]{1,0:T(8,128)(4,1)S(1)} %broadcast_compare_fusion), kind=kOutput, calls=%fused_computation.331 | convolution fusion | flops 8584960 | bytes 4494336 | tf_op jit(solution)/shard_map/bkgd,btkd->bkgt/dot_general | solution.py:38
  38.8 1.7 fusion.142
  40.5 1.5 copy.407
  42.0 4.3 %fusion.82 = f32[16,8,2,64]{3,2,1,0:T(2,128)} fusion(bf16[16,256,8,64]{1,3,2,0:T(8,128)(2,1)} %param.27, f32[16,8,2,256]{3,2,1,0:T(2,128)} %copy-done.12, pred[16,256]{1,0:T(8,128)(4,1)S(1)} %broadcast_compare_fusion, f32[16,8,2]{2,1,0:T(8,128)S(1)} %get-tuple-element.94), kind=kOutput, calls=%fused_computation.125 | convolution fusion | flops 8585216 | bytes 4527104 | tf_op jit(solution)/shard_map/bkgt,btkd->bkgd/dot_general | solution.py:44
  46.3 2.4 %copy.406 = f32[16,8,2,1]{3,2,1,0:T(2,128)} copy(f32[16,8,2,1]{2,1,0,3:T(8,128)} %bitcast.216) | data formatting | bytes 2048 | tf_op jit(solution)/shard_map/broadcast_in_dim | solution.py:96
  48.6 1.5 pad_maximum_fusion.2
  50.2 11.9 %all-gather.2 = f32[64,8,2,66]{3,1,2,0:T(8,128)S(1)} all-gather(f32[16,8,2,66]{3,1,2,0:T(8,128)S(1)} %copy.408), channel_id=4, replica_groups=mesh['dp'=2,'kv'=4] {'kv'}, dimensions={0}, use_global_device_ids=true | all-gather | bytes 337920 | tf_op jit(solution)/shard_map/all_gather | solution.py:97
  62.0 1.7 fusion.224
  68.8 1.7 copy.384
  70.5 1.7 copy.383
  72.6 10.1 %all-gather.1 = f32[64,8,2,66]{3,1,2,0:T(8,128)S(1)} all-gather(f32[16,8,2,66]{3,1,2,0:T(8,128)S(1)} %copy.385), channel_id=3, replica_groups=mesh['dp'=2,'kv'=4] {'kv'}, dimensions={0}, use_global_device_ids=true | all-gather | bytes 337920 | tf_op jit(solution)/shard_map/all_gather | solution.py:97
  82.7 1.7 fusion.223
  84.7 1.9 fusion.91
  91.1 9.4 %all-gather = f32[64,8,2,66]{3,1,2,0:T(8,128)S(1)} all-gather(f32[16,8,2,66]{3,1,2,0:T(8,128)S(1)} %copy.370), channel_id=2, replica_groups=mesh['dp'=2,'kv'=4] {'kv'}, dimensions={0}, use_global_device_ids=true | all-gather | bytes 337920 | tf_op jit(solution)/shard_map/all_gather | solution.py:97
  100.5 1.7 fusion.222
  107.4 1.8 fusion.226
  118.8 1.8 fusion.231
  121.4 1.7 fusion.105
  123.1 2.0 convolution_bitcast_fusion.1
  133.5 1.5 copy.393
  138.4 1.6 copy.392
  146.1 1.5 copy.375
  151.4 4.7 %fusion.165 = f32[16,32,128]{2,0,1:T(8,128)S(1)} fusion(bf16[32,1024,128]{2,1,0:T(8,128)(2,1)} %param.42, bf16[16,1024]{1,0:T(8,128)(2,1)S(1)} %get-tuple-element.76), kind=kOutput, calls=%fused_computation.250 | convolution fusion | flops 134217728 | bytes 8683520 | tf_op jit(solution)/shard_map/bd,edf->bef/dot_general | solution.py:65
  156.2 4.7 %fusion.161 = f32[16,32,128]{2,0,1:T(8,128)S(1)} fusion(bf16[32,1024,128]{2,1,0:T(8,128)(2,1)} %param.42, bf16[16,1024]{1,0:T(8,128)(2,1)S(1)} %get-tuple-element.77), kind=kOutput, calls=%fused_computation.247 | convolution fusion | flops 134217728 | bytes 8683520 | tf_op jit(solution)/shard_map/bd,edf->bef/dot_general | solution.py:65
  163.8 8.9 %fusion.32 = f32[16,1024]{1,0:T(8,128)} fusion(bf16[32,128,1024]{2,1,0:T(8,128)(2,1)} %param.44, bf16[32,1024,128]{2,1,0:T(8,128)(2,1)} %param.43, f32[16,32,128]{2,0,1:T(8,128)S(1)} %fusion.165, f32[16,32]{0,1:T(8,128)S(1)} %copy.380, bf16[16,1024]{1,0:T(8,128)(2,1)S(1)} %get-tuple-element.76), kind=kOutput, calls=%fused_computation.51 | convolution fusion | flops 268926976 | bytes 17139712 | tf_op jit(solution)/shard_map/bef,efd->bd/dot_general | solution.py:68
  172.7 8.7 %fusion.38 = f32[16,1024]{1,0:T(8,128)} fusion(bf16[32,128,1024]{2,1,0:T(8,128)(2,1)} %param.44, bf16[32,1024,128]{2,1,0:T(8,128)(2,1)} %param.43, f32[16,32,128]{2,0,1:T(8,128)S(1)} %fusion.161, f32[16,32]{0,1:T(8,128)S(1)} %copy.403, bf16[16,1024]{1,0:T(8,128)(2,1)S(1)} %get-tuple-element.77), kind=kOutput, calls=%fused_computation.57 | convolution fusion | flops 268926976 | bytes 17139712 | tf_op jit(solution)/shard_map/bef,efd->bd/dot_general | solution.py:68
  181.4 8.7 %fusion.44 = f32[16,1024]{1,0:T(8,128)} fusion(bf16[32,128,1024]{2,1,0:T(8,128)(2,1)} %param.44, bf16[32,1024,128]{2,1,0:T(8,128)(2,1)} %param.43, f32[16,32,128]{2,0,1:T(8,128)S(1)} %fusion.157, f32[16,32]{0,1:T(8,128)S(1)} %copy.425, bf16[16,1024]{1,0:T(8,128)(2,1)S(1)} %get-tuple-element.78), kind=kOutput, calls=%fused_computation.63 | convolution fusion | flops 268926976 | bytes 17139712 | tf_op jit(solution)/shard_map/bef,efd->bd/dot_general | solution.py:68
  190.8 26.2 %all-reduce.3.cloned.1.call-done = (f32[16,1024]{1,0:T(8,128)}, f32[16,1024]{1,0:T(8,128)}, f32[16,1024]{1,0:T(8,128)}) async-done(((f32[16,1024]{1,0:T(8,128)}, f32[16,1024]{1,0:T(8,128)}, f32[16,1024]{1,0:T(8,128)}), (f32[16,1024]{1,0:T(8,128)}, f32[16,1024]{1,0:T(8,128)}, f32[16,1024]{1,0:T(8,128)})) %all-reduce.3.cloned.1.call-update) | async-done | bytes 196624 | tf_op jit(solution)/shard_map/psum | solution.py:108
  (274 shorter events, 73.5 us)
Async XLA Ops:
  7.2 123.6 %copy-start = (bf16[1024,1024]{1,0:T(8,128)(2,1)S(1)}, bf16[1024,1024]{1,0:T(8,128)(2,1)}, u32[]{:S(2)}) copy-start(bf16[1024,1024]{1,0:T(8,128)(2,1)} %param.37) | copy-start | bytes 6291460
  7.2 14.3 %copy-start.4 = (bf16[2,16,1024]{2,1,0:T(8,128)(2,1)S(1)}, bf16[2,16,1024]{2,1,0:T(8,128)(2,1)}, u32[]{:S(2)}) copy-start(bf16[2,16,1024]{2,1,0:T(8,128)(2,1)} %param.25) | copy-start | bytes 196612
  7.2 9.0 %copy-start.26 = (f32[1024]{0:T(1024)S(1)}, f32[1024]{0:T(1024)}, u32[]{:S(2)}) copy-start(f32[1024]{0:T(1024)} %param.29) | copy-start | bytes 12292
  7.2 14.2 %copy-start.2 = (bf16[1024,512]{1,0:T(8,128)(2,1)S(1)}, bf16[1024,512]{1,0:T(8,128)(2,1)}, u32[]{:S(2)}) copy-start(bf16[1024,512]{1,0:T(8,128)(2,1)} %param.33) | copy-start | bytes 3145732
  7.2 14.2 %copy-start.41 = (f32[512]{0:T(512)S(1)}, f32[512]{0:T(512)}, u32[]{:S(2)}) copy-start(f32[512]{0:T(512)} %param.34) | copy-start | bytes 6148
  7.3 209.7 %all-reduce.3.cloned.1.call-start = ((), (), s32[]{:S(2)}) async-start(), calls=%async_computation | async-start | bytes 393216 | tf_op jit(solution)/shard_map/psum | solution.py:108
  8.4 11.4 %copy-start.45 = (f32[16]{0:T(128)}, f32[16]{0:T(128)S(1)}, u32[]{:S(2)}) copy-start(f32[16]{0:T(128)S(1)} %get-tuple-element.109) | copy-start | bytes 196
  8.4 15.4 %copy-start.43 = (f32[16]{0:T(128)}, f32[16]{0:T(128)S(1)}, u32[]{:S(2)}) copy-start(f32[16]{0:T(128)S(1)} %get-tuple-element.108) | copy-start | bytes 196
  27.1 9.4 %copy-start.24 = (f32[16,8,2,64]{3,2,1,0:T(2,128)S(1)}, f32[16,8,2,64]{3,2,1,0:T(2,128)}, u32[]{:S(2)}) copy-start(f32[16,8,2,64]{3,2,1,0:T(2,128)} %reshape.468) | copy-start | bytes 196612
  42.0 22.8 %copy-start.3 = (bf16[1024,512]{1,0:T(8,128)(2,1)S(1)}, bf16[1024,512]{1,0:T(8,128)(2,1)}, u32[]{:S(2)}) copy-start(bf16[1024,512]{1,0:T(8,128)(2,1)} %param.35) | copy-start | bytes 3145732
  42.0 22.8 %copy-start.42 = (f32[512]{0:T(512)S(1)}, f32[512]{0:T(512)}, u32[]{:S(2)}) copy-start(f32[512]{0:T(512)} %param.36) | copy-start | bytes 6148
  42.0 22.8 %copy-start.46 = (f32[16]{0:T(128)S(1)}, f32[16]{0:T(128)}, u32[]{:S(2)}) copy-start(f32[16]{0:T(128)} %copy-done.45) | copy-start | bytes 196
  42.0 22.8 %copy-start.50 = (f32[16]{0:T(128)S(1)}, f32[16]{0:T(128)}, u32[]{:S(2)}) copy-start(f32[16]{0:T(128)} %copy-done.49) | copy-start | bytes 196
  46.2 19.4 %copy-start.44 = (f32[16]{0:T(128)S(1)}, f32[16]{0:T(128)}, u32[]{:S(2)}) copy-start(f32[16]{0:T(128)} %copy-done.43) | copy-start | bytes 196
  46.2 19.4 %copy-start.52 = (f32[16]{0:T(128)S(1)}, f32[16]{0:T(128)}, u32[]{:S(2)}) copy-start(f32[16]{0:T(128)} %copy-done.51) | copy-start | bytes 196
  46.3 21.3 %copy-start.9 = (f32[16,8,2,256]{3,2,1,0:T(2,128)S(1)}, f32[16,8,2,256]{3,2,1,0:T(2,128)}, u32[]{:S(2)}) copy-start(f32[16,8,2,256]{3,2,1,0:T(2,128)} %copy-done.8) | copy-start | bytes 786436
  48.6 18.9 %copy-start.17 = (f32[16,8,2]{2,1,0:T(8,128)S(1)}, f32[16,8,2]{2,1,0:T(8,128)}, u32[]{:S(2)}) copy-start(f32[16,8,2]{2,1,0:T(8,128)} %copy-done.16) | copy-start | bytes 3076
  48.6 18.9 %copy-start.59 = (bf16[16,256,8,64]{1,3,2,0:T(8,128)(2,1)S(1)}, bf16[16,256,8,64]{1,3,2,0:T(8,128)(2,1)}, u32[]{:S(2)}) copy-start(bf16[16,256,8,64]{1,3,2,0:T(8,128)(2,1)} %param.27) | copy-start | bytes 12582916
  67.5 17.1 %copy-start.11 = (f32[16,8,2,256]{3,2,1,0:T(2,128)S(1)}, f32[16,8,2,256]{3,2,1,0:T(2,128)}, u32[]{:S(2)}) copy-start(f32[16,8,2,256]{3,2,1,0:T(2,128)} %copy-done.10) | copy-start | bytes 786436
  67.6 17.1 %copy-start.19 = (f32[16,8,2]{2,1,0:T(8,128)S(1)}, f32[16,8,2]{2,1,0:T(8,128)}, u32[]{:S(2)}) copy-start(f32[16,8,2]{2,1,0:T(8,128)} %copy-done.18) | copy-start | bytes 3076
  72.3 12.4 %copy-start.60 = (bf16[16,256,8,64]{1,3,2,0:T(8,128)(2,1)S(1)}, bf16[16,256,8,64]{1,3,2,0:T(8,128)(2,1)}, u32[]{:S(2)}) copy-start(bf16[16,256,8,64]{1,3,2,0:T(8,128)(2,1)} %param.27) | copy-start | bytes 12582916
  84.7 19.1 %copy-start.13 = (f32[16,8,64]{2,1,0:T(8,128)S(1)}, f32[16,8,64]{2,1,0:T(8,128)}, u32[]{:S(2)}) copy-start(f32[16,8,64]{2,1,0:T(8,128)} %reshape.467) | copy-start | bytes 98308
  84.7 19.2 %copy-start.14 = (f32[16,8,64]{2,1,0:T(8,128)S(1)}, f32[16,8,64]{2,1,0:T(8,128)}, u32[]{:S(2)}) copy-start(f32[16,8,64]{2,1,0:T(8,128)} %reshape.471) | copy-start | bytes 98308
  84.7 19.3 %copy-start.7 = (f32[16,8,64]{2,1,0:T(8,128)S(1)}, f32[16,8,64]{2,1,0:T(8,128)}, u32[]{:S(2)}) copy-start(f32[16,8,64]{2,1,0:T(8,128)} %reshape.461) | copy-start | bytes 98308
  86.6 20.7 %copy-start.28 = (f32[16,1,8,64]{3,2,1,0:T(8,128)S(1)}, f32[16,1,8,64]{3,2,1,0:T(8,128)}, u32[]{:S(2)}) copy-start(f32[16,1,8,64]{3,2,1,0:T(8,128)} %reshape.470) | copy-start | bytes 98308
  86.6 20.7 %copy-start.35 = (f32[16,64]{1,0:T(8,128)S(1)}, f32[16,64]{1,0:T(8,128)}, u32[]{:S(2)}) copy-start(f32[16,64]{1,0:T(8,128)} %copy-done.34) | copy-start | bytes 12292
  86.6 20.7 %copy-start.37 = (f32[16,64]{1,0:T(8,128)S(1)}, f32[16,64]{1,0:T(8,128)}, u32[]{:S(2)}) copy-start(f32[16,64]{1,0:T(8,128)} %copy-done.36) | copy-start | bytes 12292
  141.4 9.7 %copy-start.54 = (f32[1024]{0:T(1024)S(1)}, f32[1024]{0:T(1024)}, u32[]{:S(2)}) copy-start(f32[1024]{0:T(1024)} %param.40) | copy-start | bytes 12292
  141.5 9.7 %copy-start.55 = (f32[1024]{0:T(1024)S(1)}, f32[1024]{0:T(1024)}, u32[]{:S(2)}) copy-start(f32[1024]{0:T(1024)} %param.39) | copy-start | bytes 12292
  141.5 9.7 %copy-start.57 = (f32[16]{0:T(128)S(1)}, f32[16]{0:T(128)}, u32[]{:S(2)}) copy-start(f32[16]{0:T(128)} %copy-done.56) | copy-start | bytes 196
  141.5 9.7 %copy-start.58 = (f32[16]{0:T(128)S(1)}, f32[16]{0:T(128)}, u32[]{:S(2)}) copy-start(f32[16]{0:T(128)} %add_rsqrt_fusion) | copy-start | bytes 196
  151.3 9.8 %slice-start = ((s8[8388608]{0:T(1024)(128)(4,1)}), s8[4194304]{0:T(1024)(128)(4,1)S(1)}, s32[]{:S(2)}) async-start(s8[8388608]{0:T(1024)(128)(4,1)} %bitcast.204), calls=%async_computation.1 | async-start | bytes 8388608
  (32 other events, 134.9 us)
Sparse Core Ops, SparseCore 0:
  190.2 26.6 all-reduce.2
where the time goes:
time: 229 us; the launch traced here: 227 us
  matrix products  73.2 us (32%)
  local copies, waits for them, and re-layouts  42.5 us (19%)
  other arithmetic  38.7 us (17%)
  blocking collectives  31.4 us (14%)
  waiting for transfers between devices  26.2 us (11%)
  between operations  15 us (7%)
    all_gather x3, blocking collectives, layer_steps(): gathered = lax.all_gather(packed, 'kv')  31.4 us
    dot_general x3, matrix products, expert_part(): jnp.einsum('bef,efd->bd', mixed_act, w_down, preferred_element_type=jnp.f...  26.3 us
    psum x1, waiting for transfers between devices, layer_steps(): moe_sum = lax.psum(moe_part.astype(jnp.float32), 'kv')  26.2 us
    dot_general x5, matrix products, partial_stats(): jnp.einsum('bkgt,btkd->bkgd', weights.astype(jnp.bfloat16), values, prefe...  10.7 us
    dot_general x3, matrix products, expert_part(): jnp.einsum('bd,edf->bef', h_moe, w_gate, preferred_element_type=jnp.float32)  10.7 us
    dot_general x6, matrix products, partial_stats(): jnp.einsum('bkgd,btkd->bkgt', q_grp, keys, preferred_element_type=jnp.flo...  9.27 us
    convert_element_type x12, local copies, waits for them, and re-layouts, rotate_heads(): x_f32 = x_in.astype(jnp.float32)  9.12 us
    dot_general x3, matrix products, layer_steps(): jnp.dot(h_norm, w_q, preferred_element_type=jnp.float32) + b_q  6.73 us
  transfers between devices with their start and end apart: 1, of which 1 were waited for; matrix products, arithmetic and copies ran while one was open for 0% of the time, Pallas kernels for 0%

commit v1 on v0

v1 whole, which is shorter than its diff:
```python
import functools
import math

import jax
import jax.numpy as jnp
import numpy as np
from jax import lax
from jax.experimental import pallas as pl
from jax.experimental.pallas import tpu as pltpu
from jax.sharding import PartitionSpec as P

ROPE_BASE = 10000.0
ROPE_MSCALE = math.sqrt(1.0 + math.log(32.0) / math.log(4096.0))
NORM_EPS = 1e-5
NEG_FILL = -1e30
F32 = jnp.float32
BF16 = jnp.bfloat16

S = 3
B = 16
D = 1024
T = 256
KV = 8
HD = 64
E = 32
FS = 128
R = S * B
NCH = 2
CW = D // NCH
HW = CW // 2

NSMALL = 16
L_SMALL = 0
L_WQ = L_SMALL + NSMALL
L_K = L_WQ + 4
L_V = L_K + 4
L_WKV = L_V + 4
L_WO = L_WKV + 4
L_GU = L_WO + 16
L_DN = L_GU + 16
L_OUT = L_DN + 8
NLOCAL = L_OUT + 4

R_ML = 0
R_O = 3
R_C = 5
R_G = 7
R_A = 9
R_B = R_A + NCH
R_Y = R_B + NCH
NREMOTE = R_Y + NCH


def mm(a, b):
    return jnp.dot(a, b, preferred_element_type=F32)


def mm_t(a, b):
    return lax.dot_general(a, b, (((1,), (1,)), ((), ())), preferred_element_type=F32)


def norm_rows(x, gain, bias):
    mean = jnp.mean(x, axis=-1, keepdims=True)
    cen = x - mean
    var = jnp.mean(cen * cen, axis=-1, keepdims=True)
    return (cen * lax.rsqrt(var + NORM_EPS) * gain + bias).astype(BF16)


def lane_iota(shape):
    return lax.broadcasted_iota(jnp.int32, shape, len(shape) - 1)


def kernel(
    x_first, next_emb, k_hbm, v_hbm, seq_hbm, g1_h, b1_h, wq_h, bq_h, wk_h, bk_h, wv_h, bv_h, wo_h, bo_h, g2_h, b2_h,
    wr_h, wg_h, wu_h, wd_h, lf_h, idx_h, rm_h, base_h,
    hid_out, tk_out, tv_out,
    xb, g1, b1, wq, bq, wk, bk, wv, bv, wo, bo, g2, b2, wr, wg, wu, wd, lf, idx, rm, base, seq_s, kc, vc,
    qbuf, kbuf, vbuf, sbuf, wbuf, mlb, mlall, obuf, orecv, c2, ex, ga, gb, tl, oall, xm4, gx, ub, pb, ab, s2, yb, hb, tkb, tvb,
    lsem, ssem, rsem,
):
    me = lax.axis_index("kv")
    core = me % 2
    chip = me // 2
    partner = me + 1 - 2 * core
    peer = (me + 2) % 4
    diag = (partner + 2) % 4

    def local(src, dst, i):
        return pltpu.make_async_copy(src, dst, lsem.at[i])

    def remote(src, dst, i, dev):
        return pltpu.make_async_remote_copy(
            src_ref=src, dst_ref=dst, send_sem=ssem.at[i], recv_sem=rsem.at[i],
            device_id={"kv": dev}, device_id_type=pl.DeviceIdType.MESH)

    first = [
        local(x_first, xb.at[0], 0), local(next_emb, xb.at[pl.ds(1, 2)], 1), local(g1_h, g1, 2), local(b1_h, b1, 3),
        local(bq_h, bq, 4), local(lf_h, lf, 5), local(base_h, base, 6), local(seq_hbm, seq_s, 7),
    ]
    later = [
        local(bk_h, bk, 8), local(bv_h, bv, 9), local(bo_h, bo, 10), local(g2_h, g2, 11), local(b2_h, b2, 12),
        local(wr_h, wr, 13), local(idx_h, idx, 14), local(rm_h, rm, 15),
    ]
    cp_wq = [local(wq_h.at[pl.ds(i * 256, 256)], wq.at[pl.ds(i * 256, 256)], L_WQ + i) for i in range(4)]
    cp_k = [local(k_hbm.at[pl.ds(i * 4, 4)], kc.at[pl.ds(i * 4, 4)], L_K + i) for i in range(4)]

    def v_part(i):
        half = (1 - core) if i < 2 else core
        sl = (pl.ds(half * 8, 8), pl.ds((i % 2) * 4, 4))
        return local(v_hbm.at[sl], vc.at[sl], L_V + i)

    cp_v = [v_part(i) for i in range(4)]
    cp_wkv = []
    for n, (h, v) in enumerate(((wk_h, wk), (wv_h, wv))):
        for i in range(2):
            cp_wkv.append(local(h.at[pl.ds(i * 512, 512)], v.at[pl.ds(i * 512, 512)], L_WKV + 2 * n + i))
    cp_wo = [
        local(wo_h.at[pl.ds(kv * 128 + g * 64, 64)], wo.at[g, pl.ds(kv * 64, 64)], L_WO + 2 * kv + g)
        for kv in range(KV) for g in range(2)
    ]

    def gu_copies(i):
        sl = pl.ds(i * 4, 4)
        return local(wg_h.at[sl], wg.at[sl], L_GU + 2 * i), local(wu_h.at[sl], wu.at[sl], L_GU + 2 * i + 1)

    def dn_copy(i):
        sl = pl.ds(i * 4, 4)
        return local(wd_h.at[sl], wd.at[sl], L_DN + i)

    for c in first + cp_wq + cp_k:
        c.start()
    bar = pltpu.get_barrier_semaphore()
    for dev in (partner, peer, diag):
        pl.semaphore_signal(bar, inc=1, device_id={"kv": dev}, device_id_type=pl.DeviceIdType.MESH)
    for c in cp_v + later + cp_wkv + cp_wo:
        c.start()
    for i in range(8):
        for c in gu_copies(i):
            c.start()
    for i in range(8):
        dn_copy(i).start()

    qbuf[:, 6:8, :] = jnp.zeros((B, 2, 512), F32)

    for c in first:
        c.wait()

    lane48 = lane_iota((R, 128))
    inv = 1.0 / (jnp.concatenate([lf[...]] * 4, axis=1) * base[...])
    row_b = lax.broadcasted_iota(jnp.int32, (B, 128), 0)
    len_rows = jnp.zeros((B, 128), jnp.int32)
    for b in range(B):
        len_rows = jnp.where(row_b == b, seq_s[b], len_rows)
    angles = jnp.concatenate([(len_rows + s).astype(F32) for s in range(S)], axis=0) * inv
    cosv = jnp.cos(angles) * ROPE_MSCALE
    sinv = jnp.sin(angles) * ROPE_MSCALE
    low_half = (lane48 % HD) < (HD // 2)

    def rope(x):
        xf = x.astype(BF16).astype(F32)
        rot = jnp.where(low_half, -pltpu.roll(xf, 96, 1), pltpu.roll(xf, 32, 1))
        return (xf * cosv + rot * sinv).astype(BF16).astype(F32)

    h1 = norm_rows(xb[...].reshape(R, D).astype(F32), g1[...], b1[...])

    for c in cp_wq:
        c.wait()
    q = mm(h1, wq[...]) + bq[...]
    left = lane48 < HD
    for p in range(4):
        qa = rope(q[:, p * 256:p * 256 + 128]) * 0.125
        qb_ = rope(q[:, p * 256 + 128:p * 256 + 256]) * 0.125
        pair = (jnp.where(left, qa, pltpu.roll(qb_, 64, 1)), jnp.where(left, pltpu.roll(qa, 64, 1), qb_))
        for g in range(2):
            for s in range(S):
                qbuf[:, 2 * s + g, p * 128:(p + 1) * 128] = pair[g][s * B:(s + 1) * B]

    rowq = lax.broadcasted_iota(jnp.int32, (32, T), 0)
    laneq = lane_iota((32, T))
    diag_mask = (rowq // 8) == (laneq // HD)
    pos = laneq + me * T
    lane8 = lane_iota((8, 128))

    def scores(b):
        qv = qbuf[b]
        for hh in range(2):
            rep = jnp.concatenate([qv[:, hh * 256:(hh + 1) * 256]] * 4, axis=0)
            lhs = jnp.where(diag_mask, rep, 0.0).astype(BF16)
            sbuf[b, hh] = mm(lhs, kc[b, hh * 4:(hh + 1) * 4].reshape(256, T))

    def soft(b, acc):
        keep = pos < seq_s[b]
        for hh in range(2):
            sc = jnp.where(keep, sbuf[b, hh], NEG_FILL)
            m = jnp.max(sc, axis=1, keepdims=True)
            w = jnp.where(keep, jnp.exp(sc - m), 0.0)
            l = jnp.sum(w, axis=1, keepdims=True)
            wbuf[b, hh] = w.astype(BF16)
            for j in range(4):
                at = (b % 8) * 16 + hh * 4 + j
                acc = jnp.where(lane8 == at, m[j * 8:(j + 1) * 8], acc)
                acc = jnp.where(lane8 == at + 8, l[j * 8:(j + 1) * 8], acc)
        return acc

    acc = [jnp.zeros((8, 128), F32)] * 2
    for c in range(5):
        if c < 4:
            cp_k[c].wait()
            for b in range(c * 4, c * 4 + 4):
                scores(b)
        if c > 0:
            for b in range(c * 4 - 4, c * 4):
                acc[b // 8] = soft(b, acc[b // 8])
    mlb[0] = acc[0]
    mlb[1] = acc[1]
    mlall[me] = mlb[core]

    pl.semaphore_wait(bar, 3)
    send_ml = [
        remote(mlb.at[1 - core], mlall.at[me], R_ML, partner), remote(mlb.at[core], mlall.at[me], R_ML + 1, peer),
        remote(mlb.at[1 - core], mlall.at[me], R_ML + 2, diag),
    ]
    for c in send_ml:
        c.start()

    left8 = lane8 < HD

    def values(half, i, hh):
        b = half * 8 + i
        pv = mm_t(wbuf[b, hh], vc[b, hh * 4:(hh + 1) * 4].reshape(256, T))
        obuf[half, hh, i, :, 0:128] = jnp.where(left8, pv[0:8, 0:128], pv[8:16, 0:128])
        obuf[half, hh, i, :, 128:256] = jnp.where(left8, pv[16:24, 128:256], pv[24:32, 128:256])

    send_o = [remote(obuf.at[1 - core, hh], orecv.at[hh], R_O + hh, partner) for hh in range(2)]
    for hh in range(2):
        cp_v[hh].wait()
        for i in range(8):
            values(1 - core, i, hh)
        send_o[hh].start()
    for hh in range(2):
        cp_v[2 + hh].wait()
        for i in range(8):
            values(core, i, hh)

    send_ml[0].wait()
    ml_a = mlall[me]
    ml_b = mlall[partner]
    m_ab = jnp.maximum(ml_a, ml_b)
    f_a = jnp.exp(ml_a - m_ab)
    f_b = jnp.exp(ml_b - m_ab)
    pick = (lane8 // HD)

    def spread(v, i, p):
        return jnp.take_along_axis(v, pick + (i * 16 + 2 * p), axis=1, mode="promise_in_bounds")

    send_c = [remote(c2.at[hh, chip, pl.ds(0, 6)], c2.at[hh, chip, pl.ds(0, 6)], R_C + hh, peer) for hh in range(2)]
    for hh in range(2):
        send_o[hh].wait()
        for i in range(8):
            oa = obuf[core, hh, i]
            ob = orecv[hh, i]
            for p in range(2):
                ln = slice(p * 128, (p + 1) * 128)
                c2[hh, chip, :, i, ln] = (
                    oa[:, ln] * spread(f_a, i, 2 * hh + p) + ob[:, ln] * spread(f_b, i, 2 * hh + p))
        send_c[hh].start()

    for c in later + cp_wkv:
        c.wait()
    kn = mm(h1, wk[...]) + bk[...]
    vn = (mm(h1, wv[...]) + bv[...]).astype(BF16)
    for p in range(4):
        ln = slice(p * 128, (p + 1) * 128)
        kr = rope(kn[:, ln])
        for s in range(S):
            kbuf[s, :, ln] = kr[s * B:(s + 1) * B]
    for s in range(S):
        vbuf[s] = vn[s * B:(s + 1) * B].astype(F32)
        tkb[s] = kbuf[s].astype(BF16)
        tvb[s] = vn[s * B:(s + 1) * B]
    cp_tail = [local(tkb, tk_out, L_OUT), local(tvb, tv_out, L_OUT + 1)]
    for c in cp_tail:
        c.start()

    rows = pl.ds(pl.multiple_of(core * 8, 8), 8)
    kt = [kbuf[t, rows, :] for t in range(S)]
    vt = [vbuf[t, rows, :] for t in range(S)]
    trip = [(s, g, t) for s in range(S) for g in range(2) for t in range(s + 1)]
    prod = jnp.concatenate([qbuf[rows, 2 * s + g, :] * kt[t] for s, g, t in trip], axis=0)
    hi = prod.astype(BF16)
    lo = (prod - hi.astype(F32)).astype(BF16)
    r2 = lax.broadcasted_iota(jnp.int32, (256, 128), 0)
    ones = jnp.where(((r2 % 128) // HD) == (lane_iota((256, 128)) // HD), 1.0, 0.0).astype(BF16)
    tsc = jnp.concatenate(
        [mm(jnp.concatenate([hi[:, p * 128:(p + 1) * 128], lo[:, p * 128:(p + 1) * 128]], axis=1), ones) for p in range(4)], axis=1)

    for c in send_ml[1:]:
        c.wait()
    ml = [mlall[d] for d in range(4)]
    for ch in range(2):
        a, b_ = ml[2 * ch], ml[2 * ch + 1]
        mc = jnp.maximum(a, b_)
        lc = (pltpu.roll(a, 120, 1) * jnp.exp(a - mc) + pltpu.roll(b_, 120, 1) * jnp.exp(b_ - mc))
        for i in range(8):
            for p in range(4):
                ln = slice(p * 128, (p + 1) * 128)
                ex[2 * ch, :, i, ln] = spread(mc, i, p)
                ex[2 * ch + 1, :, i, ln] = spread(lc, i, p)

    for s in range(S):
        for g in range(2):
            j = 2 * s + g
            sc = [tsc[n * 8:(n + 1) * 8] for n, key in enumerate(trip) if key[:2] == (s, g)]
            mt = functools.reduce(jnp.maximum, sc)
            wt = [jnp.exp(v - mt) for v in sc]
            lt = functools.reduce(jnp.add, wt)
            ot = functools.reduce(jnp.add, [w.astype(BF16).astype(F32) * v for w, v in zip(wt, vt)])
            m0, l0, m1, l1 = ex[0, j], ex[1, j], ex[2, j], ex[3, j]
            top = jnp.maximum(jnp.maximum(m0, m1), mt)
            f0, f1, ft = jnp.exp(m0 - top), jnp.exp(m1 - top), jnp.exp(mt - top)
            inv_l = 1.0 / (l0 * f0 + l1 * f1 + lt * ft)
            ga[j] = f0 * inv_l
            gb[j] = f1 * inv_l
            tl[j] = ot * (ft * inv_l)

    send_g = [remote(oall.at[core, hh], oall.at[core, hh], R_G + hh, partner) for hh in range(2)]
    for hh in range(2):
        send_c[hh].wait()
        ln = slice(hh * 256, (hh + 1) * 256)
        for j in range(6):
            oall[core, hh, j] = c2[hh, 0, j] * ga[j][:, ln] + c2[hh, 1, j] * gb[j][:, ln] + tl[j][:, ln]
        send_g[hh].start()

    for c in cp_wo:
        c.wait()
    for c in send_g:
        c.wait()
    att = None
    for g in range(2):
        o_g = jnp.concatenate([
            jnp.concatenate([jnp.concatenate([oall[h, hh, 2 * s + g] for hh in range(2)], axis=1) for h in range(2)], axis=0)
            for s in range(S)], axis=0).astype(BF16)
        part = mm(o_g, wo[g])
        att = part if att is None else att + part
    xm = (xb[...].reshape(R, D).astype(F32) + att + bo[...]).astype(BF16).astype(F32)
    for n in range(NCH):
        for h in range(2):
            xm4[n, h] = xm[:, n * CW + h * HW:n * CW + (h + 1) * HW]
    h2 = norm_rows(xm, g2[...], b2[...])

    logits = mm_t(h2, wr[...])
    eye = jnp.where(lax.broadcasted_iota(jnp.int32, (B, B), 0) == lane_iota((B, B)), 1.0, 0.0)
    picks = jnp.concatenate([mm_t(eye, idx[s].astype(F32)) for s in range(S)], axis=0)
    lane_e = lane_iota((R, E)).astype(F32)
    gates = jnp.zeros((R, E), F32)
    for k in range(8):
        on = jnp.concatenate([rm[s, :, k, :] for s in range(S)], axis=0) == 1
        mk = jnp.where(on, logits, NEG_FILL)
        pk = jnp.exp(mk - jnp.max(mk, axis=1, keepdims=True))
        pk = pk / jnp.sum(pk, axis=1, keepdims=True)
        gates = gates + jnp.where(picks[:, k:k + 1] == lane_e, pk, 0.0)
    for e in range(E):
        gx[e] = jnp.broadcast_to(gates[:, e:e + 1], (R, 128))

    def gu_body(i, carry):
        for c in gu_copies(i):
            c.wait()
        for n in range(4):
            e = i * 4 + n
            both = mm(h2, jnp.concatenate([wg[e], wu[e]], axis=1))
            a, up = both[:, :FS], both[:, FS:]
            ub[e] = (gx[e] * (a * (1.0 / (1.0 + jnp.exp(-a)))) * up).astype(BF16)
        return carry

    lax.fori_loop(0, 8, gu_body, 0)

    for i in range(8):
        dn_copy(i).wait()
    u = jnp.concatenate([ub[e] for e in range(E)], axis=1)
    send_a = [remote(pb.at[n, 1 - core], ab.at[n], R_A + n, partner) for n in range(NCH)]
    send_b = [remote(s2.at[n, chip], s2.at[n, chip], R_B + n, peer) for n in range(NCH)]
    send_y = [remote(yb.at[n, core], yb.at[n, core], R_Y + n, partner) for n in range(NCH)]
    for n in range(NCH):
        part = mm(u, wd[:, :, n * CW:(n + 1) * CW].reshape(E * FS, CW)).astype(BF16).astype(F32)
        pb[n, 0] = part[:, :HW]
        pb[n, 1] = part[:, HW:]
        send_a[n].start()
    for n in range(NCH):
        send_a[n].wait()
        s2[n, chip] = pb[n, core] + ab[n]
        send_b[n].start()
    for n in range(NCH):
        send_b[n].wait()
        yb[n, core] = xm4[n, core] + (s2[n, 0] + s2[n, 1])
        send_y[n].start()
    for n in range(NCH):
        send_y[n].wait()
        for h in range(2):
            hb[:, :, n * CW + h * HW:n * CW + (h + 1) * HW] = yb[n, h].astype(BF16).reshape(S, B, HW)
    cp_h = local(hb, hid_out, L_OUT + 2)
    cp_h.start()
    for c in cp_tail:
        c.wait()
    cp_h.wait()


def solution(mesh):
    def layer_steps(x_first, next_emb, k_cache, v_cache, seq_len, ln1_gain, ln1_bias, w_q, b_q, w_k, b_k, w_v, b_v, w_o, b_o, ln2_gain, ln2_bias, w_router, w_gate, w_up, w_down, long_factor, expert_idx, route_mask):
        def row(v):
            return v.reshape(1, -1)

        powers = (np.float32(ROPE_BASE) ** (np.arange(32, dtype=np.float32) * np.float32(2.0) / np.float32(HD))).astype(np.float32)
        base = jnp.asarray(np.tile(powers, 4)[None, :])
        args = (
            x_first, next_emb, jnp.transpose(k_cache, (0, 2, 3, 1)), jnp.transpose(v_cache, (0, 2, 3, 1)), seq_len,
            row(ln1_gain), row(ln1_bias), w_q, row(b_q), w_k, row(b_k), w_v, row(b_v), w_o, row(b_o), row(ln2_gain), row(ln2_bias),
            jnp.transpose(w_router), w_gate, w_up, w_down, row(long_factor), jnp.transpose(expert_idx, (0, 2, 1)), route_mask, base,
        )
        V = pltpu.VMEM
        scratch = [
            V((S, B, D), BF16), V((1, D), F32), V((1, D), F32), V((D, D), BF16), V((1, D), F32), V((D, 512), BF16), V((1, 512), F32),
            V((D, 512), BF16), V((1, 512), F32), V((2, 512, D), BF16), V((1, D), F32), V((1, D), F32), V((1, D), F32), V((E, D), BF16),
            V((E, D, FS), BF16), V((E, D, FS), BF16), V((E, FS, D), BF16), V((1, 32), F32), V((S, 8, B), jnp.int32),
            V((S, B, 8, E), jnp.int32), V((1, 128), F32), pltpu.SMEM((B,), jnp.int32), V((B, KV, HD, T), BF16), V((B, KV, HD, T), BF16),
            V((B, 8, 512), F32), V((S, B, 512), F32), V((S, B, 512), F32), V((B, 2, 32, T), F32), V((B, 2, 32, T), BF16),
            V((2, 8, 128), F32), V((4, 8, 128), F32), V((2, 2, 8, 8, 256), F32), V((2, 8, 8, 256), F32), V((2, 2, 8, 8, 256), F32),
            V((4, 8, 8, 512), F32), V((6, 8, 512), F32), V((6, 8, 512), F32), V((6, 8, 512), F32), V((2, 2, 6, 8, 256), F32),
            V((NCH, 2, R, HW), F32), V((E, R, 128), F32), V((E, R, FS), BF16), V((NCH, 2, R, HW), F32), V((NCH, R, HW), F32),
            V((NCH, 2, R, HW), F32), V((NCH, 2, R, HW), F32), V((S, B, D), BF16), V((S, B, 512), BF16), V((S, B, 512), BF16),
            pltpu.SemaphoreType.DMA((NLOCAL,)), pltpu.SemaphoreType.DMA((NREMOTE,)), pltpu.SemaphoreType.DMA((NREMOTE,)),
        ]
        anyspec = pl.BlockSpec(memory_space=pl.ANY)
        hid, tk, tv = pl.pallas_call(
            kernel,
            out_shape=(
                jax.ShapeDtypeStruct((S, B, D), BF16), jax.ShapeDtypeStruct((S, B, 512), BF16), jax.ShapeDtypeStruct((S, B, 512), BF16)),
            in_specs=[anyspec] * len(args),
            out_specs=(anyspec,) * 3,
            scratch_shapes=scratch,
            compiler_params=pltpu.CompilerParams(collective_id=0, has_side_effects=True, vmem_limit_bytes=60 * 1024 * 1024),
        )(*args)

        def tail(v):
            return jnp.transpose(v.reshape(S, B, KV, HD), (1, 0, 2, 3))

        return hid, tail(tk), tail(tv)

    replicated = P()
    in_specs = (P('dp'), P(None, 'dp'), P('dp', 'kv'), P('dp', 'kv'), P('dp')) + (replicated,) * 13 + (P(None, None, 'kv'), P(None, None, 'kv'), P(None, 'kv'), replicated, P(None, 'dp'), P(None, 'dp'))
    out_specs = (P(None, 'dp'), P('dp'), P('dp'))
    return jax.shard_map(layer_steps, mesh=mesh, in_specs=in_specs, out_specs=out_specs, check_vma=False)
```

time: 229 us -> 30.3 us (0.13)
  matrix products: 73.2 us -> 0 us
  other arithmetic: 38.7 us -> 0 us
  local copies, waits for them, and re-layouts: 42.5 us -> 4.09 us
  blocking collectives: 31.4 us -> 0 us
  waiting for transfers between devices: 26.2 us -> 0 us
  Pallas kernels: 0 us -> 25.4 us
  between operations: 15 us -> 0.66 us
    dot_general x32 -> x0, matrix products: 73.2 us -> none  [the longest x3 26.3 us: expert_part(): jnp.einsum('bef,efd->bd', mixed_act, w_down, preferred_element_type=jnp.f...]
    all_gather x3 -> x0, blocking collectives: 31.4 us -> none  [layer_steps(): gathered = lax.all_gather(packed, 'kv')]
    psum x1 -> x0, waiting for transfers between devices: 26.2 us -> none  [layer_steps(): moe_sum = lax.psum(moe_part.astype(jnp.float32), 'kv')]
    pallas_call x0 -> x1, Pallas kernels: none -> 25.4 us  [layer_steps(): pl.pallas_call(kernel, out_shape=(jax.ShapeDtypeStruct((S, B, D), BF16),...]
    broadcast_in_dim x11 -> x0, local copies, waits for them, and re-layouts: 12.5 us -> none  [the longest x3 4.97 us: layer_steps(): run_max[..., None]]
    reduce_sum x16 -> x0, other arithmetic: 11 us -> none  [the longest x3 4.72 us: partial_stats(): run_sum = jnp.sum(weights, axis=-1)]
    convert_element_type x18 -> x0, local copies, waits for them, and re-layouts: 9.62 us -> none  [the longest x12 9.12 us: rotate_heads(): x_f32 = x_in.astype(jnp.float32)]
    slice x9 -> x0, local copies, waits for them, and re-layouts: 9.31 us -> none  [the longest x3 4.48 us: layer_steps(): sum_all = jnp.concatenate([gathered[..., 1], tail_sum[None]], axis=0)]
  transfers between devices with their start and end apart: 1 -> 0, of which waited for: 1 -> 0; matrix products, arithmetic and copies ran while one was open for 0% -> 0% of each run, Pallas kernels for 0% -> 0%
where the time goes in v1:
time: 30.3 us; the launch traced here: 30.1 us
  Pallas kernels  25.4 us (84%)
  local copies, waits for them, and re-layouts  4.09 us (13%)
  between operations  0.66 us (2%)
    pallas_call x1, Pallas kernels, layer_steps(): pl.pallas_call(kernel, out_shape=(jax.ShapeDtypeStruct((S, B, D), BF16),...  25.4 us
    reshape x2, local copies, waits for them, and re-layouts, tail(): return jnp.transpose(v.reshape(S, B, KV, HD), (1, 0, 2, 3))  1.84 us
    unnamed x1, local copies, waits for them, and re-layouts  1.54 us
    transpose x1, local copies, waits for them, and re-layouts, tail(): return jnp.transpose(v.reshape(S, B, KV, HD), (1, 0, 2, 3))  0.71 us

profile of v1, /device:TPU:0, one launch (start us, length us, event | category | flops | bytes accessed | tf_op | source)
XLA Modules:
  0.0 30.1 jit_solution(16009596132225111014)
XLA Ops:
  0.6 25.4 %shard_map.256 = (bf16[3,16,1024]{2,1,0:T(8,128)(2,1)}, bf16[3,16,512]{2,1,0:T(8,128)(2,1)}, bf16[3,16,512]{2,1,0:T(8,128)(2,1)}) custom-call(bf16[16,1024]{1,0:T(8,128)(2,1)} %x_first.1, bf16[2,16,1024]{2,1,0:T(8,128)(2,1)} %next_emb.1, bf16[16,8,64,256]{3,2,1,0:T(8,128)(2,1)} %bitcast.17, bf16[16,8,64,256]{3,2,1,0:T(8,128)(2,1)} %bitcast.18, s32[16]{0:T(128)} %seq_hbm.1, ...), custom_call_target="tpu_custom_call" | custom-call | tf_op jit(solution)/shard_map/pallas_call | solution.py:433
  26.0 0.9 %reshape.48 = bf16[3,16,8,64]{3,2,1,0:T(8,128)(2,1)S(1)} reshape(bf16[3,16,512]{2,1,0:T(8,128)(2,1)} %get-tuple-element.7) | data formatting | bytes 98304 | tf_op jit(solution)/shard_map/reshape | solution.py:444
  26.9 0.9 %reshape.49 = bf16[3,16,8,64]{3,2,1,0:T(8,128)(2,1)S(1)} reshape(bf16[3,16,512]{2,1,0:T(8,128)(2,1)} %get-tuple-element.8) | data formatting | bytes 98304 | tf_op jit(solution)/shard_map/reshape | solution.py:444
  27.9 0.7 %copy_bitcast_fusion = (bf16[16,3,8,64]{3,2,1,0:T(8,128)(2,1)}, bf16[16,3,8,64]{3,2,1,0:T(8,128)(2,1)}) fusion(bf16[3,16,8,64]{3,2,1,0:T(8,128)(2,1)S(1)} %reshape.49, bf16[3,16,8,64]{3,2,1,0:T(8,128)(2,1)S(1)} %reshape.48), kind=kLoop, calls=%fused_computation | loop fusion | bytes 196608 | tf_op jit(solution)/shard_map/transpose | solution.py:444
  28.6 1.5 %copy.33 = bf16[3,16,1024]{2,1,0:T(8,128)(2,1)} copy(bf16[3,16,1024]{2,1,0:T(8,128)(2,1)} %get-tuple-element.14) | data formatting | bytes 196608

commit v2 on v1

v2 whole, which is shorter than its diff:
```python
import functools
import itertools
import math

import jax
import jax.numpy as jnp
import numpy as np
from jax import lax
from jax.experimental import pallas as pl
from jax.experimental.pallas import tpu as pltpu
from jax.sharding import PartitionSpec as P

ROPE_BASE = 10000.0
ROPE_MSCALE = math.sqrt(1.0 + math.log(32.0) / math.log(4096.0))
NORM_EPS = 1e-5
NEG_FILL = -1e30
F32 = jnp.float32
BF16 = jnp.bfloat16

S = 3
B = 16
D = 1024
T = 256
KV = 8
HD = 64
E = 32
FS = 128
R = S * B
NCH = 4
CW = D // NCH
HW = CW // 2

SMALL, PARTS, GROUPS = 16, 4, 8
L_SMALL, L_WQ, L_K, L_V, L_WKV, L_WO, L_GU, L_DN, NLOCAL = itertools.accumulate(
    (SMALL, PARTS, PARTS, PARTS, PARTS, 2 * KV, 2 * GROUPS, GROUPS), initial=0)
R_ML, R_O, R_C, R_G, R_A, R_B, R_Y, NREMOTE = itertools.accumulate((3, 2, 2, 2, NCH, NCH, NCH), initial=0)
LN = 128
HALF = 8


def at(i, width=LN):
    return slice(i * width, (i + 1) * width)


def mm(a, b):
    return jnp.dot(a, b, preferred_element_type=F32)


def mm_t(a, b):
    return lax.dot_general(a, b, (((1,), (1,)), ((), ())), preferred_element_type=F32)


def norm_rows(x, gain, bias):
    mean = jnp.mean(x, axis=-1, keepdims=True)
    cen = x - mean
    var = jnp.mean(cen * cen, axis=-1, keepdims=True)
    return (cen * lax.rsqrt(var + NORM_EPS) * gain + bias).astype(BF16)


def lane_iota(shape):
    return lax.broadcasted_iota(jnp.int32, shape, len(shape) - 1)


def kernel(
    x_first, next_emb, k_hbm, v_hbm, seq_hbm, g1_h, b1_h, wq_h, bq_h, wk_h, bk_h, wv_h, bv_h, wo_h, bo_h, g2_h, b2_h,
    wr_h, wg_h, wu_h, wd_h, lf_h, idx_h, rm_h, base_h,
    hb, tkb, tvb,
    xb, g1, b1, wq, bq, wk, bk, wv, bv, wo, bo, g2, b2, wr, wg, wu, wd, lf, idx, rm, base, seq_s, kc, vc,
    qbuf, kbuf, vbuf, sbuf, wbuf, mlb, mlall, obuf, orecv, c2, ex, ga, gb, tl, oall, xm4, gx, raw, qraw, dsum, ub, pb, ab, s2, yb, tkf, tvf,
    lsem, ssem, rsem,
):
    me = lax.axis_index("kv")
    core = me % 2
    chip = me // 2
    partner = me + 1 - 2 * core
    peer = (me + 2) % 4
    diag = (partner + 2) % 4

    def local(src, dst, i):
        return pltpu.make_async_copy(src, dst, lsem.at[i])

    def remote(src, dst, i, dev):
        return pltpu.make_async_remote_copy(
            src_ref=src, dst_ref=dst, send_sem=ssem.at[i], recv_sem=rsem.at[i],
            device_id={"kv": dev}, device_id_type=pl.DeviceIdType.MESH)

    small = [
        local(src, dst, i) for i, (src, dst) in enumerate((
            (x_first, xb.at[0]), (next_emb, xb.at[pl.ds(1, S - 1)]), (g1_h, g1), (b1_h, b1), (bq_h, bq), (lf_h, lf), (base_h, base),
            (seq_hbm, seq_s), (bk_h, bk), (bv_h, bv), (bo_h, bo), (g2_h, g2), (b2_h, b2), (wr_h, wr), (idx_h, idx), (rm_h, rm)))
    ]
    first, later = small[:HALF], small[HALF:]
    cp_wq = [local(wq_h.at[:, pl.ds(i * T, T)], wq.at[:, pl.ds(i * T, T)], L_WQ + i) for i in range(4)]
    other, own = (1 - core) * 8, core * 8

    def k_part(i):
        sl = pl.ds((other if i < 2 else own) + (i % 2) * 4, 4)
        return local(k_hbm.at[sl], kc.at[sl], L_K + i)

    def v_part(i):
        sl = (pl.ds(other if i < 2 else own, 8), pl.ds((i % 2) * 4, 4))
        return local(v_hbm.at[sl], vc.at[sl], L_V + i)

    cp_k = [k_part(i) for i in range(4)]
    cp_v = [v_part(i) for i in range(4)]
    cp_wkv = []
    for n, (h, v) in enumerate(((wk_h, wk), (wv_h, wv))):
        for i in range(2):
            cp_wkv.append(local(h.at[pl.ds(i * 512, 512)], v.at[pl.ds(i * 512, 512)], L_WKV + 2 * n + i))
    cp_wo = [
        local(wo_h.at[pl.ds(kv * 128 + g * 64, 64)], wo.at[g, pl.ds(kv * 64, 64)], L_WO + 2 * kv + g)
        for kv in range(KV) for g in range(2)
    ]

    def gu_copies(i):
        sl = pl.ds(i * 4, 4)
        return local(wg_h.at[sl], wg.at[sl], L_GU + 2 * i), local(wu_h.at[sl], wu.at[sl], L_GU + 2 * i + 1)

    def dn_copy(i):
        sl = pl.ds(i * 4, 4)
        return local(wd_h.at[sl], wd.at[sl], L_DN + i)

    for c in first + cp_wq + cp_k:
        c.start()
    bar = pltpu.get_barrier_semaphore()
    for dev in (partner, peer, diag):
        pl.semaphore_signal(bar, inc=1, device_id={"kv": dev}, device_id_type=pl.DeviceIdType.MESH)
    qbuf[:, 6:8, :] = jnp.zeros((B, 2, 512), F32)

    for c in first:
        c.wait()
    for c in cp_v:
        c.start()

    lane48 = lane_iota((R, 128))
    inv = 1.0 / (jnp.concatenate([lf[...]] * 4, axis=1) * base[...])
    row_b = lax.broadcasted_iota(jnp.int32, (B, 128), 0)
    len_rows = jnp.zeros((B, 128), jnp.int32)
    for b in range(B):
        len_rows = jnp.where(row_b == b, seq_s[b], len_rows)
    angles = jnp.concatenate([(len_rows + s).astype(F32) for s in range(S)], axis=0) * inv
    cosv = jnp.cos(angles) * ROPE_MSCALE
    sinv = jnp.sin(angles) * ROPE_MSCALE
    low_half = (lane48 % HD) < (HD // 2)

    def rope(x):
        xf = x.astype(BF16).astype(F32)
        rot = jnp.where(low_half, -pltpu.roll(xf, 96, 1), pltpu.roll(xf, 32, 1))
        return (xf * cosv + rot * sinv).astype(BF16).astype(F32)

    h1 = norm_rows(xb[...].reshape(R, D).astype(F32), g1[...], b1[...])

    left = lane48 < HD

    def put_q(q, p):
        qa = rope(q[:, :128]) * 0.125
        qb_ = rope(q[:, 128:]) * 0.125
        pair = (jnp.where(left, qa, pltpu.roll(qb_, 64, 1)), jnp.where(left, pltpu.roll(qa, 64, 1), qb_))
        for g in range(2):
            for s in range(S):
                qbuf[:, 2 * s + g, at(p)] = pair[g][at(s, B)]

    cp_wq[0].wait()
    cp_wq[1].wait()
    q_lo = mm(h1, wq[:, :512]) + bq[:, :512]
    qraw[...] = q_lo
    cp_wq[2].wait()
    cp_wq[3].wait()
    for c in later + cp_wo + cp_wkv:
        c.start()
    q_hi = mm(h1, wq[:, 512:]) + bq[:, 512:]
    for p in range(4):
        put_q(qraw[:, p * 256:(p + 1) * 256] if p < 2 else q_hi[:, (p - 2) * 256:(p - 1) * 256], p)

    rowq = lax.broadcasted_iota(jnp.int32, (32, T), 0)
    laneq = lane_iota((32, T))
    diag_mask = (rowq // 8) == (laneq // HD)
    pos = laneq + me * T
    lane8 = lane_iota((8, 128))

    def scores(start, i):
        qv = qbuf[start + i]
        for hh in range(2):
            rep = jnp.concatenate([qv[:, at(hh, T)]] * 4, axis=0)
            lhs = jnp.where(diag_mask, rep, 0.0).astype(BF16)
            sbuf[start + i, hh] = mm(lhs, kc[start + i, at(hh, 4)].reshape(256, T))

    def soft(start, i, acc):
        keep = pos < seq_s[start + i]
        for hh in range(2):
            sc = jnp.where(keep, sbuf[start + i, hh], NEG_FILL)
            m = jnp.max(sc, axis=1, keepdims=True)
            w = jnp.where(keep, jnp.exp(sc - m), 0.0)
            l = jnp.sum(w, axis=1, keepdims=True)
            wbuf[start + i, hh] = w.astype(BF16)
            for j in range(4):
                spot = i * 16 + hh * 4 + j
                acc = jnp.where(lane8 == spot, m[at(j, 8)], acc)
                acc = jnp.where(lane8 == spot + 8, l[at(j, 8)], acc)
        return acc

    left8 = lane8 < HD

    def values(half, i, hh):
        b = half * 8 + i
        pv = mm_t(wbuf[b, hh], vc[b, at(hh, 4)].reshape(256, T))
        obuf[half, hh, i, :, 0:128] = jnp.where(left8, pv[0:8, 0:128], pv[8:16, 0:128])
        obuf[half, hh, i, :, 128:256] = jnp.where(left8, pv[16:24, 128:256], pv[24:32, 128:256])

    send_ml = [
        remote(mlb.at[1 - core], mlall.at[me], R_ML, partner), remote(mlb.at[core], mlall.at[me], R_ML + 1, peer),
        remote(mlb.at[1 - core], mlall.at[me], R_ML + 2, diag),
    ]
    send_o = [remote(obuf.at[1 - core, hh], orecv.at[hh], R_O + hh, partner) for hh in range(2)]
    zero = jnp.zeros((8, 128), F32)

    cp_k[0].wait()
    for i in range(4):
        scores(other, i)
    cp_k[1].wait()
    for i in range(4):
        scores(other, 4 + i)
    acc = zero
    for i in range(4):
        acc = soft(other, i, acc)
    cp_k[2].wait()
    for i in range(8):
        for c in gu_copies(i):
            c.start()
    for i in range(4):
        scores(own, i)
    for i in range(4):
        acc = soft(other, 4 + i, acc)
    mlb[1 - core] = acc
    pl.semaphore_wait(bar, 3)
    send_ml[0].start()
    send_ml[2].start()

    cp_v[0].wait()
    cp_k[3].wait()
    for i in range(8):
        values(1 - core, i, 0)
    for i in range(4):
        scores(own, 4 + i)
    acc = zero
    for i in range(4):
        acc = soft(own, i, acc)
    send_o[0].start()
    cp_v[1].wait()
    for i in range(8):
        dn_copy(i).start()
    for i in range(8):
        values(1 - core, i, 1)
    for i in range(4):
        acc = soft(own, 4 + i, acc)
    mlb[core] = acc
    mlall[me] = acc
    send_o[1].start()
    send_ml[1].start()

    pick = (lane8 // HD)

    def spread(v, i, p):
        return jnp.take_along_axis(v, pick + (i * 16 + 2 * p), axis=1, mode="promise_in_bounds")

    send_c = [remote(c2.at[hh, chip, pl.ds(0, 6)], c2.at[hh, chip, pl.ds(0, 6)], R_C + hh, peer) for hh in range(2)]
    for hh in range(2):
        cp_v[2 + hh].wait()
        for i in range(8):
            values(core, i, hh)
        if hh == 0:
            send_ml[0].wait()
            ml_a = mlall[me]
            ml_b = mlall[partner]
            m_ab = jnp.maximum(ml_a, ml_b)
            f_a = jnp.exp(ml_a - m_ab)
            f_b = jnp.exp(ml_b - m_ab)
        send_o[hh].wait()
        for i in range(8):
            oa = obuf[core, hh, i]
            ob = orecv[hh, i]
            for p in range(2):
                ln = at(p)
                c2[hh, chip, :, i, ln] = (
                    oa[:, ln] * spread(f_a, i, 2 * hh + p) + ob[:, ln] * spread(f_b, i, 2 * hh + p))
        send_c[hh].start()

    for c in later + cp_wkv:
        c.wait()
    kn = mm(h1, wk[...]) + bk[...]
    vn = (mm(h1, wv[...]) + bv[...]).astype(BF16)
    vn = vn.astype(F32)
    for p in range(4):
        ln = at(p)
        for val, buf, fin in ((rope(kn[:, ln]), kbuf, tkf), (vn[:, ln], vbuf, tvf)):
            swap = pltpu.roll(val, 64, 1)
            for s in range(S):
                r = at(s, B)
                buf[s, :, ln] = val[r]
                fin[:, s, 2 * p, :] = val[r, :HD]
                fin[:, s, 2 * p + 1, :] = swap[r, :HD]
    tkb[...] = tkf[...].astype(BF16)
    tvb[...] = tvf[...].astype(BF16)

    rows = pl.ds(pl.multiple_of(core * 8, 8), 8)
    kt = [kbuf[t, rows, :] for t in range(S)]
    vt = [vbuf[t, rows, :] for t in range(S)]
    trip = [(s, g, t) for s in range(S) for g in range(2) for t in range(s + 1)]
    prod = jnp.concatenate([qbuf[rows, 2 * s + g, :] * kt[t] for s, g, t in trip], axis=0)
    hi = prod.astype(BF16)
    lo = (prod - hi.astype(F32)).astype(BF16)
    r2 = lax.broadcasted_iota(jnp.int32, (256, 128), 0)
    ones = jnp.where(((r2 % 128) // HD) == (lane_iota((256, 128)) // HD), 1.0, 0.0).astype(BF16)
    tsc = jnp.concatenate(
        [mm(jnp.concatenate([hi[:, at(p)], lo[:, at(p)]], axis=1), ones) for p in range(4)], axis=1)

    for c in send_ml[1:]:
        c.wait()
    ml = [mlall[d] for d in range(4)]
    for ch in range(2):
        a, b_ = ml[2 * ch], ml[2 * ch + 1]
        mc = jnp.maximum(a, b_)
        lc = (pltpu.roll(a, 120, 1) * jnp.exp(a - mc) + pltpu.roll(b_, 120, 1) * jnp.exp(b_ - mc))
        for i in range(8):
            for p in range(4):
                ln = at(p)
                ex[2 * ch, :, i, ln] = spread(mc, i, p)
                ex[2 * ch + 1, :, i, ln] = spread(lc, i, p)

    for s in range(S):
        for g in range(2):
            j = 2 * s + g
            sc = [tsc[at(n, 8)] for n, key in enumerate(trip) if key[:2] == (s, g)]
            mt = functools.reduce(jnp.maximum, sc)
            wt = [jnp.exp(v - mt) for v in sc]
            lt = functools.reduce(jnp.add, wt)
            ot = functools.reduce(jnp.add, [w.astype(BF16).astype(F32) * v for w, v in zip(wt, vt)])
            m0, l0, m1, l1 = ex[0, j], ex[1, j], ex[2, j], ex[3, j]
            top = jnp.maximum(jnp.maximum(m0, m1), mt)
            f0, f1, ft = jnp.exp(m0 - top), jnp.exp(m1 - top), jnp.exp(mt - top)
            inv_l = 1.0 / (l0 * f0 + l1 * f1 + lt * ft)
            ga[j] = f0 * inv_l
            gb[j] = f1 * inv_l
            tl[j] = ot * (ft * inv_l)

    send_g = [remote(oall.at[core, hh], oall.at[core, hh], R_G + hh, partner) for hh in range(2)]
    for hh in range(2):
        send_c[hh].wait()
        ln = at(hh, T)
        for j in range(6):
            oall[core, hh, j] = c2[hh, 0, j] * ga[j][:, ln] + c2[hh, 1, j] * gb[j][:, ln] + tl[j][:, ln]
        send_g[hh].start()

    for c in cp_wo:
        c.wait()
    att = None
    for hh in range(2):
        send_g[hh].wait()
        for g in range(2):
            o_g = jnp.concatenate([oall[h, hh, 2 * s + g] for s in range(S) for h in range(2)], axis=0).astype(BF16)
            part = mm(o_g, wo[g, at(hh, T)])
            att = part if att is None else att + part
    xm = (xb[...].reshape(R, D).astype(F32) + att + bo[...]).astype(BF16).astype(F32)
    for n in range(NCH):
        for h in range(2):
            xm4[n, h] = xm[:, at(2 * n + h, HW)]
    h2 = norm_rows(xm, g2[...], b2[...])

    def act(i):
        for n in range(4):
            e = i * 4 + n
            raw[e] = mm(h2, jnp.concatenate([wg[e], wu[e]], axis=1))

    def mix(i):
        for n in range(4):
            e = i * 4 + n
            a, up = raw[e, :, :FS], raw[e, :, FS:]
            ub[e] = (gx[e] * (a * (1.0 / (1.0 + jnp.exp(-a)))) * up).astype(BF16)

    for i in range(8):
        for c in gu_copies(i):
            c.wait()
        dn_copy(i).wait()
    logits = mm_t(h2, wr[...])
    act(0)
    act(1)
    eye = jnp.where(lax.broadcasted_iota(jnp.int32, (B, B), 0) == lane_iota((B, B)), 1.0, 0.0)
    picks = jnp.concatenate([mm_t(eye, idx[s].astype(F32)) for s in range(S)], axis=0)
    lane_e = lane_iota((R, E)).astype(F32)
    gates = jnp.zeros((R, E), F32)
    for k in range(8):
        on = jnp.concatenate([rm[s, :, k, :] for s in range(S)], axis=0) == 1
        mk = jnp.where(on, logits, NEG_FILL)
        pk = jnp.exp(mk - jnp.max(mk, axis=1, keepdims=True))
        pk = pk / jnp.sum(pk, axis=1, keepdims=True)
        gates = gates + jnp.where(picks[:, k:k + 1] == lane_e, pk, 0.0)
    for e in range(E):
        gx[e] = jnp.broadcast_to(gates[:, e:e + 1], (R, 128))

    for i in range(2, 8):
        act(i)
        mix(i - 2)
    mix(6)
    mix(7)

    half = E * FS // 2

    def copy_a(n):
        return remote(pb.at[n, 1 - core], ab.at[n], R_A + n, partner)

    def down(n, carry):
        u = jnp.concatenate([ub[e] for e in range(E)], axis=1)
        wn = wd[:, :, pl.ds(pl.multiple_of(n * CW, CW), CW)].reshape(E * FS, CW)
        dsum[0] = mm(u[:, :half], wn[:half])
        dsum[1] = mm(u[:, half:], wn[half:])
        part = (dsum[0] + dsum[1]).astype(BF16).astype(F32)
        pb[n, 0] = part[:, :HW]
        pb[n, 1] = part[:, HW:]
        copy_a(n).start()
        return carry

    lax.fori_loop(0, NCH, down, 0)
    send_a = [copy_a(n) for n in range(NCH)]
    send_b = [remote(s2.at[n, chip], s2.at[n, chip], R_B + n, peer) for n in range(NCH)]
    send_y = [remote(yb.at[n, core], yb.at[n, core], R_Y + n, partner) for n in range(NCH)]
    for n in range(NCH):
        send_a[n].wait()
        s2[n, chip] = pb[n, core] + ab[n]
        send_b[n].start()
    for n in range(NCH):
        send_b[n].wait()
        yb[n, core] = xm4[n, core] + (s2[n, 0] + s2[n, 1])
        send_y[n].start()
    for n in range(NCH):
        send_y[n].wait()
        for h in range(2):
            hb[:, :, at(2 * n + h, HW)] = yb[n, h].astype(BF16).reshape(S, B, HW)


def write_kernel(h, tk, tv, h_out, tk_out, tv_out, sem):
    copies = [pltpu.make_async_copy(a, b, sem.at[i]) for i, (a, b) in enumerate(((h, h_out), (tk, tk_out), (tv, tv_out)))]
    for c in copies:
        c.start()
    for c in copies:
        c.wait()


def solution(mesh):
    def layer_steps(x_first, next_emb, k_cache, v_cache, seq_len, ln1_gain, ln1_bias, w_q, b_q, w_k, b_k, w_v, b_v, w_o, b_o, ln2_gain, ln2_bias, w_router, w_gate, w_up, w_down, long_factor, expert_idx, route_mask):
        def row(v):
            return v.reshape(1, -1)

        powers = (np.float32(ROPE_BASE) ** (np.arange(32, dtype=np.float32) * np.float32(2.0) / np.float32(HD))).astype(np.float32)
        base = jnp.asarray(np.tile(powers, 4)[None, :])
        args = (
            x_first, next_emb, jnp.transpose(k_cache, (0, 2, 3, 1)), jnp.transpose(v_cache, (0, 2, 3, 1)), seq_len,
            row(ln1_gain), row(ln1_bias), w_q, row(b_q), w_k, row(b_k), w_v, row(b_v), w_o, row(b_o), row(ln2_gain), row(ln2_bias),
            jnp.transpose(w_router), w_gate, w_up, w_down, row(long_factor), jnp.transpose(expert_idx, (0, 2, 1)), route_mask, base,
        )
        V = pltpu.VMEM
        scratch = [
            V((S, B, D), BF16), V((1, D), F32), V((1, D), F32), V((D, D), BF16), V((1, D), F32), V((D, 512), BF16), V((1, 512), F32),
            V((D, 512), BF16), V((1, 512), F32), V((2, 512, D), BF16), V((1, D), F32), V((1, D), F32), V((1, D), F32), V((E, D), BF16),
            V((E, D, FS), BF16), V((E, D, FS), BF16), V((E, FS, D), BF16), V((1, 32), F32), V((S, 8, B), jnp.int32),
            V((S, B, 8, E), jnp.int32), V((1, 128), F32), pltpu.SMEM((B,), jnp.int32), V((B, KV, HD, T), BF16), V((B, KV, HD, T), BF16),
            V((B, 8, 512), F32), V((S, B, 512), F32), V((S, B, 512), F32), V((B, 2, 32, T), F32), V((B, 2, 32, T), BF16),
            V((2, 8, 128), F32), V((4, 8, 128), F32), V((2, 2, 8, 8, 256), F32), V((2, 8, 8, 256), F32), V((2, 2, 8, 8, 256), F32),
            V((4, 8, 8, 512), F32), V((6, 8, 512), F32), V((6, 8, 512), F32), V((6, 8, 512), F32), V((2, 2, 6, 8, 256), F32),
            V((NCH, 2, R, HW), F32), V((E, R, 128), F32), V((E, R, 2 * FS), F32), V((R, 512), F32), V((2, R, CW), F32), V((E, R, FS), BF16), V((NCH, 2, R, HW), F32), V((NCH, R, HW), F32),
            V((NCH, 2, R, HW), F32), V((NCH, 2, R, HW), F32), V((B, S, KV, HD), F32), V((B, S, KV, HD), F32),
            pltpu.SemaphoreType.DMA((NLOCAL,)), pltpu.SemaphoreType.DMA((NREMOTE,)), pltpu.SemaphoreType.DMA((NREMOTE,)),
        ]
        anyspec = pl.BlockSpec(memory_space=pl.ANY)
        outs = [((S, B, D), BF16), ((B, S, KV, HD), BF16), ((B, S, KV, HD), BF16)]
        vmem = pl.BlockSpec(memory_space=pltpu.VMEM)
        parts = pl.pallas_call(
            kernel,
            out_shape=tuple(V(*o) for o in outs),
            in_specs=[anyspec] * len(args),
            out_specs=(vmem,) * 3,
            scratch_shapes=scratch,
            compiler_params=pltpu.CompilerParams(collective_id=0, has_side_effects=True, vmem_limit_bytes=60 * 1024 * 1024),
        )(*args)
        return pl.pallas_call(
            write_kernel,
            out_shape=tuple(jax.ShapeDtypeStruct(*o) for o in outs),
            in_specs=[vmem] * 3,
            out_specs=(anyspec,) * 3,
            scratch_shapes=[pltpu.SemaphoreType.DMA((3,))],
            compiler_params=pltpu.CompilerParams(vmem_limit_bytes=1024 * 1024),
        )(*parts)

    replicated = P()
    in_specs = (P('dp'), P(None, 'dp'), P('dp', 'kv'), P('dp', 'kv'), P('dp')) + (replicated,) * 13 + (P(None, None, 'kv'), P(None, None, 'kv'), P(None, 'kv'), replicated, P(None, 'dp'), P(None, 'dp'))
    out_specs = (P(None, 'dp'), P('dp'), P('dp'))
    return jax.shard_map(layer_steps, mesh=mesh, in_specs=in_specs, out_specs=out_specs, check_vma=False)
```

time: 30.3 us -> 27.5 us (0.908)
  local copies, waits for them, and re-layouts: 4.09 us -> 0 us
  Pallas kernels: 25.4 us -> 26.8 us
    reshape x2 -> x0, local copies, waits for them, and re-layouts: 1.84 us -> none  [tail(): return jnp.transpose(v.reshape(S, B, KV, HD), (1, 0, 2, 3))]
    unnamed x1 -> x0, local copies, waits for them, and re-layouts: 1.54 us -> none
    pallas_call x1 -> x2, Pallas kernels: 25.4 us -> 26.8 us  [the longest x1 26 us: layer_steps(): pl.pallas_call(kernel, out_shape=tuple((V(*o) for o in outs)), in_specs=[...]
    transpose x1 -> x0, local copies, waits for them, and re-layouts: 0.71 us -> none  [tail(): return jnp.transpose(v.reshape(S, B, KV, HD), (1, 0, 2, 3))]
where the time goes in v2:
time: 27.5 us; the launch traced here: 27.4 us
  Pallas kernels  26.8 us (97%)
  between operations  0.65 us (2%)
    pallas_call x1, Pallas kernels, layer_steps(): pl.pallas_call(kernel, out_shape=tuple((V(*o) for o in outs)), in_specs=[...  26 us
    pallas_call x1, Pallas kernels, layer_steps(): pl.pallas_call(write_kernel, out_shape=tuple((jax.ShapeDtypeStruct(*o) fo...  0.73 us

profile of v2, /device:TPU:0, one launch (start us, length us, event | category | flops | bytes accessed | tf_op | source)
XLA Modules:
  0.0 27.4 jit_solution(4583573283932191367)
XLA Ops:
  0.6 26.0 %shard_map.256 = (bf16[3,16,1024]{2,1,0:T(8,128)(2,1)S(1)}, bf16[16,3,8,64]{3,2,1,0:T(8,128)(2,1)S(1)}, bf16[16,3,8,64]{3,2,1,0:T(8,128)(2,1)S(1)}) custom-call(bf16[16,1024]{1,0:T(8,128)(2,1)} %x_first.1, bf16[2,16,1024]{2,1,0:T(8,128)(2,1)} %next_emb.1, bf16[16,8,64,256]{3,2,1,0:T(8,128)(2,1)} %bitcast.13, bf16[16,8,64,256]{3,2,1,0:T(8,128)(2,1)} %bitcast.14, ...), custom_call_target="tpu_custom_call" | custom-call | tf_op jit(solution)/shard_map/pallas_call | solution.py:476
  26.7 0.7 %shard_map.257 = (bf16[3,16,1024]{2,1,0:T(8,128)(2,1)}, bf16[16,3,8,64]{3,2,1,0:T(8,128)(2,1)}, bf16[16,3,8,64]{3,2,1,0:T(8,128)(2,1)}) custom-call(bf16[3,16,1024]{2,1,0:T(8,128)(2,1)S(1)} %get-tuple-element.6.h, bf16[16,3,8,64]{3,2,1,0:T(8,128)(2,1)S(1)} %get-tuple-element.7.tk, bf16[16,3,8,64]{3,2,1,0:T(8,128)(2,1)S(1)} %get-tuple-element.8.tv), custom_call_target="tpu_custom_call" | custom-call | tf_op jit(solution)/shard_map/pallas_call | solution.py:484

commit v3 on v2

--- a/solution.py
+++ b/solution.py
@@ -380,7 +380,6 @@
     for i in range(8):
         for c in gu_copies(i):
             c.wait()
-        dn_copy(i).wait()
     logits = mm_t(h2, wr[...])
     act(0)
     act(1)
@@ -403,6 +402,8 @@
     mix(6)
     mix(7)
 
+    for i in range(GROUPS):
+        dn_copy(i).wait()
     half = E * FS // 2
 
     def copy_a(n):

time: 27.5 us -> 25.1 us (0.913)
  Pallas kernels: 26.8 us -> 24.3 us
    pallas_call x1, Pallas kernels: 26 us -> 23.6 us  [layer_steps(): pl.pallas_call(kernel, out_shape=tuple((V(*o) for o in outs)), in_specs=[...]
where the time goes in v3:
time: 25.1 us; the launch traced here: 25 us
  Pallas kernels  24.3 us (97%)
  between operations  0.65 us (3%)
    pallas_call x1, Pallas kernels, layer_steps(): pl.pallas_call(kernel, out_shape=tuple((V(*o) for o in outs)), in_specs=[...  23.6 us
    pallas_call x1, Pallas kernels, layer_steps(): pl.pallas_call(write_kernel, out_shape=tuple((jax.ShapeDtypeStruct(*o) fo...  0.73 us

profile of v3, /device:TPU:0, one launch (start us, length us, event | category | flops | bytes accessed | tf_op | source)
XLA Modules:
  0.0 25.0 jit_solution(8303801307210411734)
XLA Ops:
  0.6 23.6 %shard_map.256 = (bf16[3,16,1024]{2,1,0:T(8,128)(2,1)S(1)}, bf16[16,3,8,64]{3,2,1,0:T(8,128)(2,1)S(1)}, bf16[16,3,8,64]{3,2,1,0:T(8,128)(2,1)S(1)}) custom-call(bf16[16,1024]{1,0:T(8,128)(2,1)} %x_first.1, bf16[2,16,1024]{2,1,0:T(8,128)(2,1)} %next_emb.1, bf16[16,8,64,256]{3,2,1,0:T(8,128)(2,1)} %bitcast.13, bf16[16,8,64,256]{3,2,1,0:T(8,128)(2,1)} %bitcast.14, ...), custom_call_target="tpu_custom_call" | custom-call | tf_op jit(solution)/shard_map/pallas_call | solution.py:477
  24.3 0.7 %shard_map.257 = (bf16[3,16,1024]{2,1,0:T(8,128)(2,1)}, bf16[16,3,8,64]{3,2,1,0:T(8,128)(2,1)}, bf16[16,3,8,64]{3,2,1,0:T(8,128)(2,1)}) custom-call(bf16[3,16,1024]{2,1,0:T(8,128)(2,1)S(1)} %get-tuple-element.6.h, bf16[16,3,8,64]{3,2,1,0:T(8,128)(2,1)S(1)} %get-tuple-element.7.tk, bf16[16,3,8,64]{3,2,1,0:T(8,128)(2,1)S(1)} %get-tuple-element.8.tv), custom_call_target="tpu_custom_call" | custom-call | tf_op jit(solution)/shard_map/pallas_call | solution.py:485

commit v4 on v2

--- a/solution.py
+++ b/solution.py
@@ -28,12 +28,12 @@
 R = S * B
 NCH = 4
 CW = D // NCH
-HW = CW // 2
-
-SMALL, PARTS, GROUPS = 16, 4, 8
-L_SMALL, L_WQ, L_K, L_V, L_WKV, L_WO, L_GU, L_DN, NLOCAL = itertools.accumulate(
-    (SMALL, PARTS, PARTS, PARTS, PARTS, 2 * KV, 2 * GROUPS, GROUPS), initial=0)
-R_ML, R_O, R_C, R_G, R_A, R_B, R_Y, NREMOTE = itertools.accumulate((3, 2, 2, 2, NCH, NCH, NCH), initial=0)
+
+GROUPS = 8
+SMALL, PARTS = 8, 4
+L_SMALL, L_WQ, L_K, L_V, L_WO, L_GU, L_DN, NLOCAL = itertools.accumulate((SMALL, 2, PARTS, PARTS, 1, 2, 1), initial=0)
+R_ML, R_O, R_C, R_G, R_P, R_B, NRECV = itertools.accumulate((3, 2, 2, 2, NCH, NCH), initial=0)
+S_ML, S_O, S_C, S_G, S_P, S_B, NSEND = range(7)
 LN = 128
 HALF = 8
 
@@ -66,7 +66,7 @@
     wr_h, wg_h, wu_h, wd_h, lf_h, idx_h, rm_h, base_h,
     hb, tkb, tvb,
     xb, g1, b1, wq, bq, wk, bk, wv, bv, wo, bo, g2, b2, wr, wg, wu, wd, lf, idx, rm, base, seq_s, kc, vc,
-    qbuf, kbuf, vbuf, sbuf, wbuf, mlb, mlall, obuf, orecv, c2, ex, ga, gb, tl, oall, xm4, gx, raw, qraw, dsum, ub, pb, ab, s2, yb, tkf, tvf,
+    qbuf, kbuf, vbuf, sbuf, wbuf, mlb, mlall, obuf, orecv, c2, ex, ga, gb, tl, oall, xm4, gx, raw, qraw, picks, ub, pb, ab, s2, yb, tkf, tvf,
     lsem, ssem, rsem,
 ):
     me = lax.axis_index("kv")
@@ -79,18 +79,18 @@
     def local(src, dst, i):
         return pltpu.make_async_copy(src, dst, lsem.at[i])
 
-    def remote(src, dst, i, dev):
+    def remote(src, dst, snd, rcv, dev):
         return pltpu.make_async_remote_copy(
-            src_ref=src, dst_ref=dst, send_sem=ssem.at[i], recv_sem=rsem.at[i],
+            src_ref=src, dst_ref=dst, send_sem=ssem.at[snd], recv_sem=rsem.at[rcv],
             device_id={"kv": dev}, device_id_type=pl.DeviceIdType.MESH)
 
     small = [
-        local(src, dst, i) for i, (src, dst) in enumerate((
+        local(src, dst, L_SMALL + i % SMALL) for i, (src, dst) in enumerate((
             (x_first, xb.at[0]), (next_emb, xb.at[pl.ds(1, S - 1)]), (g1_h, g1), (b1_h, b1), (bq_h, bq), (lf_h, lf), (base_h, base),
             (seq_hbm, seq_s), (bk_h, bk), (bv_h, bv), (bo_h, bo), (g2_h, g2), (b2_h, b2), (wr_h, wr), (idx_h, idx), (rm_h, rm)))
     ]
-    first, later = small[:HALF], small[HALF:]
-    cp_wq = [local(wq_h.at[:, pl.ds(i * T, T)], wq.at[:, pl.ds(i * T, T)], L_WQ + i) for i in range(4)]
+    first, later = small[:SMALL], small[SMALL:]
+    cp_wq = [local(wq_h.at[:, pl.ds(i * 512, 512)], wq.at[:, pl.ds(i * 512, 512)], L_WQ + i) for i in range(2)]
     other, own = (1 - core) * 8, core * 8
 
     def k_part(i):
@@ -103,22 +103,14 @@
 
     cp_k = [k_part(i) for i in range(4)]
     cp_v = [v_part(i) for i in range(4)]
-    cp_wkv = []
-    for n, (h, v) in enumerate(((wk_h, wk), (wv_h, wv))):
-        for i in range(2):
-            cp_wkv.append(local(h.at[pl.ds(i * 512, 512)], v.at[pl.ds(i * 512, 512)], L_WKV + 2 * n + i))
+    cp_wkv = [local(wk_h, wk, L_WQ), local(wv_h, wv, L_WQ + 1)]
     cp_wo = [
-        local(wo_h.at[pl.ds(kv * 128 + g * 64, 64)], wo.at[g, pl.ds(kv * 64, 64)], L_WO + 2 * kv + g)
-        for kv in range(KV) for g in range(2)
+        local(wo_h.at[pl.ds(kv * 128 + g * 64, 64)], wo.at[g, pl.ds(kv * 64, 64)], L_WO) for kv in range(KV) for g in range(2)
     ]
 
-    def gu_copies(i):
+    def up_copy(src, dst, i, sem):
         sl = pl.ds(i * 4, 4)
-        return local(wg_h.at[sl], wg.at[sl], L_GU + 2 * i), local(wu_h.at[sl], wu.at[sl], L_GU + 2 * i + 1)
-
-    def dn_copy(i):
-        sl = pl.ds(i * 4, 4)
-        return local(wd_h.at[sl], wd.at[sl], L_DN + i)
+        return local(src.at[sl], dst.at[sl], sem)
 
     for c in first + cp_wq + cp_k:
         c.start()
@@ -161,11 +153,9 @@
                 qbuf[:, 2 * s + g, at(p)] = pair[g][at(s, B)]
 
     cp_wq[0].wait()
-    cp_wq[1].wait()
     q_lo = mm(h1, wq[:, :512]) + bq[:, :512]
     qraw[...] = q_lo
-    cp_wq[2].wait()
-    cp_wq[3].wait()
+    cp_wq[1].wait()
     for c in later + cp_wo + cp_wkv:
         c.start()
     q_hi = mm(h1, wq[:, 512:]) + bq[:, 512:]
@@ -208,10 +198,10 @@
         obuf[half, hh, i, :, 128:256] = jnp.where(left8, pv[16:24, 128:256], pv[24:32, 128:256])
 
     send_ml = [
-        remote(mlb.at[1 - core], mlall.at[me], R_ML, partner), remote(mlb.at[core], mlall.at[me], R_ML + 1, peer),
-        remote(mlb.at[1 - core], mlall.at[me], R_ML + 2, diag),
+        remote(mlb.at[1 - core], mlall.at[me], S_ML, R_ML, partner), remote(mlb.at[core], mlall.at[me], S_ML, R_ML + 1, peer),
+        remote(mlb.at[1 - core], mlall.at[me], S_ML, R_ML + 2, diag),
     ]
-    send_o = [remote(obuf.at[1 - core, hh], orecv.at[hh], R_O + hh, partner) for hh in range(2)]
+    send_o = [remote(obuf.at[1 - core, hh], orecv.at[hh], S_O, R_O + hh, partner) for hh in range(2)]
     zero = jnp.zeros((8, 128), F32)
 
     cp_k[0].wait()
@@ -224,9 +214,9 @@
     for i in range(4):
         acc = soft(other, i, acc)
     cp_k[2].wait()
-    for i in range(8):
-        for c in gu_copies(i):
-            c.start()
+    for i in range(GROUPS):
+        up_copy(wg_h, wg, i, L_GU).start()
+        up_copy(wu_h, wu, i, L_GU + 1).start()
     for i in range(4):
         scores(own, i)
     for i in range(4):
@@ -247,8 +237,8 @@
         acc = soft(own, i, acc)
     send_o[0].start()
     cp_v[1].wait()
-    for i in range(8):
-        dn_copy(i).start()
+    for i in range(GROUPS):
+        up_copy(wd_h, wd, i, L_DN).start()
     for i in range(8):
         values(1 - core, i, 1)
     for i in range(4):
@@ -263,19 +253,19 @@
     def spread(v, i, p):
         return jnp.take_along_axis(v, pick + (i * 16 + 2 * p), axis=1, mode="promise_in_bounds")
 
-    send_c = [remote(c2.at[hh, chip, pl.ds(0, 6)], c2.at[hh, chip, pl.ds(0, 6)], R_C + hh, peer) for hh in range(2)]
+    send_c = [remote(c2.at[hh, chip, pl.ds(0, 6)], c2.at[hh, chip, pl.ds(0, 6)], S_C, R_C + hh, peer) for hh in range(2)]
     for hh in range(2):
         cp_v[2 + hh].wait()
         for i in range(8):
             values(core, i, hh)
         if hh == 0:
-            send_ml[0].wait()
+            send_ml[0].wait_recv()
             ml_a = mlall[me]
             ml_b = mlall[partner]
             m_ab = jnp.maximum(ml_a, ml_b)
             f_a = jnp.exp(ml_a - m_ab)
             f_b = jnp.exp(ml_b - m_ab)
-        send_o[hh].wait()
+        send_o[hh].wait_recv()
         for i in range(8):
             oa = obuf[core, hh, i]
             ob = orecv[hh, i]
@@ -314,8 +304,11 @@
     tsc = jnp.concatenate(
         [mm(jnp.concatenate([hi[:, at(p)], lo[:, at(p)]], axis=1), ones) for p in range(4)], axis=1)
 
+    eye = jnp.where(lax.broadcasted_iota(jnp.int32, (B, B), 0) == lane_iota((B, B)), 1.0, 0.0)
+    picks[...] = jnp.concatenate([mm_t(eye, idx[s].astype(F32)) for s in range(S)], axis=0)
+
     for c in send_ml[1:]:
-        c.wait()
+        c.wait_recv()
     ml = [mlall[d] for d in range(4)]
     for ch in range(2):
         a, b_ = ml[2 * ch], ml[2 * ch + 1]
@@ -343,27 +336,25 @@
             gb[j] = f1 * inv_l
             tl[j] = ot * (ft * inv_l)
 
-    send_g = [remote(oall.at[core, hh], oall.at[core, hh], R_G + hh, partner) for hh in range(2)]
+    send_g = [remote(oall.at[core, hh], oall.at[core, hh], S_G, R_G + hh, partner) for hh in range(2)]
     for hh in range(2):
-        send_c[hh].wait()
+        send_c[hh].wait_recv()
         ln = at(hh, T)
         for j in range(6):
             oall[core, hh, j] = c2[hh, 0, j] * ga[j][:, ln] + c2[hh, 1, j] * gb[j][:, ln] + tl[j][:, ln]
         send_g[hh].start()
 
-    for c in cp_wo:
-        c.wait()
+    local(wo, wo, L_WO).wait()
     att = None
     for hh in range(2):
-        send_g[hh].wait()
+        send_g[hh].wait_recv()
         for g in range(2):
             o_g = jnp.concatenate([oall[h, hh, 2 * s + g] for s in range(S) for h in range(2)], axis=0).astype(BF16)
             part = mm(o_g, wo[g, at(hh, T)])
             att = part if att is None else att + part
     xm = (xb[...].reshape(R, D).astype(F32) + att + bo[...]).astype(BF16).astype(F32)
     for n in range(NCH):
-        for h in range(2):
-            xm4[n, h] = xm[:, at(2 * n + h, HW)]
+        xm4[n] = xm[:, at(n, CW)]
     h2 = norm_rows(xm, g2[...], b2[...])
 
     def act(i):
@@ -377,64 +368,72 @@
             a, up = raw[e, :, :FS], raw[e, :, FS:]
             ub[e] = (gx[e] * (a * (1.0 / (1.0 + jnp.exp(-a)))) * up).astype(BF16)
 
-    for i in range(8):
-        for c in gu_copies(i):
-            c.wait()
-        dn_copy(i).wait()
+    local(wg, wg, L_GU).wait()
+    local(wu, wu, L_GU + 1).wait()
     logits = mm_t(h2, wr[...])
-    act(0)
-    act(1)
-    eye = jnp.where(lax.broadcasted_iota(jnp.int32, (B, B), 0) == lane_iota((B, B)), 1.0, 0.0)
-    picks = jnp.concatenate([mm_t(eye, idx[s].astype(F32)) for s in range(S)], axis=0)
+    for i in range(4):
+        act(i)
     lane_e = lane_iota((R, E)).astype(F32)
+    chosen = picks[...]
     gates = jnp.zeros((R, E), F32)
     for k in range(8):
         on = jnp.concatenate([rm[s, :, k, :] for s in range(S)], axis=0) == 1
         mk = jnp.where(on, logits, NEG_FILL)
         pk = jnp.exp(mk - jnp.max(mk, axis=1, keepdims=True))
         pk = pk / jnp.sum(pk, axis=1, keepdims=True)
-        gates = gates + jnp.where(picks[:, k:k + 1] == lane_e, pk, 0.0)
+        gates = gates + jnp.where(chosen[:, k:k + 1] == lane_e, pk, 0.0)
     for e in range(E):
         gx[e] = jnp.broadcast_to(gates[:, e:e + 1], (R, 128))
 
-    for i in range(2, 8):
+    for i in range(4, 6):
         act(i)
-        mix(i - 2)
-    mix(6)
-    mix(7)
-
-    half = E * FS // 2
-
-    def copy_a(n):
-        return remote(pb.at[n, 1 - core], ab.at[n], R_A + n, partner)
-
-    def down(n, carry):
+        mix(i - 4)
+
+    def down(m):
         u = jnp.concatenate([ub[e] for e in range(E)], axis=1)
-        wn = wd[:, :, pl.ds(pl.multiple_of(n * CW, CW), CW)].reshape(E * FS, CW)
-        dsum[0] = mm(u[:, :half], wn[:half])
-        dsum[1] = mm(u[:, half:], wn[half:])
-        part = (dsum[0] + dsum[1]).astype(BF16).astype(F32)
-        pb[n, 0] = part[:, :HW]
-        pb[n, 1] = part[:, HW:]
-        copy_a(n).start()
-        return carry
-
-    lax.fori_loop(0, NCH, down, 0)
-    send_a = [copy_a(n) for n in range(NCH)]
-    send_b = [remote(s2.at[n, chip], s2.at[n, chip], R_B + n, peer) for n in range(NCH)]
-    send_y = [remote(yb.at[n, core], yb.at[n, core], R_Y + n, partner) for n in range(NCH)]
-    for n in range(NCH):
-        send_a[n].wait()
-        s2[n, chip] = pb[n, core] + ab[n]
-        send_b[n].start()
-    for n in range(NCH):
-        send_b[n].wait()
-        yb[n, core] = xm4[n, core] + (s2[n, 0] + s2[n, 1])
-        send_y[n].start()
-    for n in range(NCH):
-        send_y[n].wait()
-        for h in range(2):
-            hb[:, :, at(2 * n + h, HW)] = yb[n, h].astype(BF16).reshape(S, B, HW)
+        part = mm(u, wd[:, :, at(m, 2 * CW)].reshape(E * FS, 2 * CW)).astype(BF16).astype(F32)
+        pb[2 * m] = part[:, :CW]
+        pb[2 * m + 1] = part[:, CW:]
+
+    send_a = [remote(pb.at[n], ab.at[n], S_P, R_P + n, partner) for n in range(NCH)]
+    send_b = [remote(s2.at[n, chip], s2.at[n, chip], S_B, R_B + n, peer) for n in range(NCH)]
+    send_y = [remote(yb.at[n], yb.at[n], S_P, R_P + n, partner) for n in range(NCH)]
+
+    local(wd, wd, L_DN).wait()
+    for i in range(6, 8):
+        act(i)
+        mix(i - 4)
+    for i in range(4, 8):
+        mix(i)
+    for m in range(2):
+        down(m)
+
+        @pl.when(core == 0)
+        def _():
+            for n in (2 * m, 2 * m + 1):
+                send_a[n].start()
+
+    @pl.when(core == 1)
+    def _():
+        for n in range(NCH):
+            send_a[n].wait_recv()
+            s2[n, chip] = ab[n] + pb[n]
+            send_b[n].start()
+        for n in range(NCH):
+            send_b[n].wait_recv()
+            yb[n] = xm4[n] + (s2[n, 0] + s2[n, 1])
+            send_y[n].start()
+            hb[:, :, at(n, CW)] = yb[n].astype(BF16).reshape(S, B, CW)
+        remote(s2.at[:, chip], s2.at[:, chip], S_B, R_B, peer).wait_send()
+
+    @pl.when(core == 0)
+    def _():
+        for n in range(NCH):
+            send_y[n].wait_recv()
+            hb[:, :, at(n, CW)] = yb[n].astype(BF16).reshape(S, B, CW)
+
+    for ref, snd in ((mlall.at[pl.ds(0, 3)], S_ML), (obuf.at[1 - core], S_O), (c2.at[:, chip, pl.ds(0, 6)], S_C), (oall.at[core], S_G), (pb, S_P)):
+        remote(ref, ref, snd, R_ML, partner).wait_send()
 
 
 def write_kernel(h, tk, tv, h_out, tk_out, tv_out, sem):
@@ -466,9 +465,9 @@
             V((B, 8, 512), F32), V((S, B, 512), F32), V((S, B, 512), F32), V((B, 2, 32, T), F32), V((B, 2, 32, T), BF16),
             V((2, 8, 128), F32), V((4, 8, 128), F32), V((2, 2, 8, 8, 256), F32), V((2, 8, 8, 256), F32), V((2, 2, 8, 8, 256), F32),
             V((4, 8, 8, 512), F32), V((6, 8, 512), F32), V((6, 8, 512), F32), V((6, 8, 512), F32), V((2, 2, 6, 8, 256), F32),
-            V((NCH, 2, R, HW), F32), V((E, R, 128), F32), V((E, R, 2 * FS), F32), V((R, 512), F32), V((2, R, CW), F32), V((E, R, FS), BF16), V((NCH, 2, R, HW), F32), V((NCH, R, HW), F32),
-            V((NCH, 2, R, HW), F32), V((NCH, 2, R, HW), F32), V((B, S, KV, HD), F32), V((B, S, KV, HD), F32),
-            pltpu.SemaphoreType.DMA((NLOCAL,)), pltpu.SemaphoreType.DMA((NREMOTE,)), pltpu.SemaphoreType.DMA((NREMOTE,)),
+            V((NCH, R, CW), F32), V((E, R, 128), F32), V((E, R, 2 * FS), F32), V((R, 512), F32), V((R, 8), F32), V((E, R, FS), BF16), V((NCH, R, CW), F32),
+            V((NCH, R, CW), F32), V((NCH, 2, R, CW), F32), V((NCH, R, CW), F32), V((B, S, KV, HD), F32), V((B, S, KV, HD), F32),
+            pltpu.SemaphoreType.DMA((NLOCAL,)), pltpu.SemaphoreType.DMA((NSEND,)), pltpu.SemaphoreType.DMA((NRECV,)),
         ]
         anyspec = pl.BlockSpec(memory_space=pl.ANY)
         outs = [((S, B, D), BF16), ((B, S, KV, HD), BF16), ((B, S, KV, HD), BF16)]

time: 27.5 us -> 24.4 us (0.89)
  Pallas kernels: 26.8 us -> 23.6 us
    pallas_call x1, Pallas kernels: 26 us -> 22.9 us  [layer_steps(): pl.pallas_call(kernel, out_shape=tuple((V(*o) for o in outs)), in_specs=[...]
where the time goes in v4:
time: 24.4 us; the launch traced here: 24.3 us
  Pallas kernels  23.6 us (97%)
  between operations  0.65 us (3%)
    pallas_call x1, Pallas kernels, layer_steps(): pl.pallas_call(kernel, out_shape=tuple((V(*o) for o in outs)), in_specs=[...  22.9 us
    pallas_call x1, Pallas kernels, layer_steps(): pl.pallas_call(write_kernel, out_shape=tuple((jax.ShapeDtypeStruct(*o) fo...  0.73 us

profile of v4, /device:TPU:0, one launch (start us, length us, event | category | flops | bytes accessed | tf_op | source)
XLA Modules:
  0.0 24.3 jit_solution(2111284120663952074)
XLA Ops:
  0.6 22.9 %shard_map.256 = (bf16[3,16,1024]{2,1,0:T(8,128)(2,1)S(1)}, bf16[16,3,8,64]{3,2,1,0:T(8,128)(2,1)S(1)}, bf16[16,3,8,64]{3,2,1,0:T(8,128)(2,1)S(1)}) custom-call(bf16[16,1024]{1,0:T(8,128)(2,1)} %x_first.1, bf16[2,16,1024]{2,1,0:T(8,128)(2,1)} %next_emb.1, bf16[16,8,64,256]{3,2,1,0:T(8,128)(2,1)} %bitcast.13, bf16[16,8,64,256]{3,2,1,0:T(8,128)(2,1)} %bitcast.14, ...), custom_call_target="tpu_custom_call" | custom-call | tf_op jit(solution)/shard_map/pallas_call | solution.py:475
  23.5 0.7 %shard_map.257 = (bf16[3,16,1024]{2,1,0:T(8,128)(2,1)}, bf16[16,3,8,64]{3,2,1,0:T(8,128)(2,1)}, bf16[16,3,8,64]{3,2,1,0:T(8,128)(2,1)}) custom-call(bf16[3,16,1024]{2,1,0:T(8,128)(2,1)S(1)} %get-tuple-element.6.h, bf16[16,3,8,64]{3,2,1,0:T(8,128)(2,1)S(1)} %get-tuple-element.7.tk, bf16[16,3,8,64]{3,2,1,0:T(8,128)(2,1)S(1)} %get-tuple-element.8.tv), custom_call_target="tpu_custom_call" | custom-call | tf_op jit(solution)/shard_map/pallas_call | solution.py:483

commit v5 on v4

--- a/solution.py
+++ b/solution.py
@@ -31,8 +31,8 @@
 
 GROUPS = 8
 SMALL, PARTS = 8, 4
-L_SMALL, L_WQ, L_K, L_V, L_WO, L_GU, L_DN, NLOCAL = itertools.accumulate((SMALL, 2, PARTS, PARTS, 1, 2, 1), initial=0)
-R_ML, R_O, R_C, R_G, R_P, R_B, NRECV = itertools.accumulate((3, 2, 2, 2, NCH, NCH), initial=0)
+L_SMALL, L_WQ, L_K, L_V, L_WO, L_GU, L_DN, NLOCAL = itertools.accumulate((SMALL, 2, PARTS, PARTS, 1, 2, 2), initial=0)
+R_ML, R_O, R_C, R_G, R_P, R_B, NRECV = itertools.accumulate((3, 2, 2, 2, NCH, NCH + 1), initial=0)
 S_ML, S_O, S_C, S_G, S_P, S_B, NSEND = range(7)
 LN = 128
 HALF = 8
@@ -66,7 +66,7 @@
     wr_h, wg_h, wu_h, wd_h, lf_h, idx_h, rm_h, base_h,
     hb, tkb, tvb,
     xb, g1, b1, wq, bq, wk, bk, wv, bv, wo, bo, g2, b2, wr, wg, wu, wd, lf, idx, rm, base, seq_s, kc, vc,
-    qbuf, kbuf, vbuf, sbuf, wbuf, mlb, mlall, obuf, orecv, c2, ex, ga, gb, tl, oall, xm4, gx, raw, qraw, picks, ub, pb, ab, s2, yb, tkf, tvf,
+    qbuf, kbuf, vbuf, sbuf, wbuf, mlb, mlall, obuf, orecv, c2, ex, ga, gb, tl, oall, xm4, gx, raw, qraw, picks, wrt, h2, ub, pb, ab, db, s2, yb, tkf, tvf,
     lsem, ssem, rsem,
 ):
     me = lax.axis_index("kv")
@@ -111,6 +111,10 @@
     def up_copy(src, dst, i, sem):
         sl = pl.ds(i * 4, 4)
         return local(src.at[sl], dst.at[sl], sem)
+
+    def down_copy(m, e, n):
+        sl = (pl.ds(e, n), pl.ds(0, FS), pl.ds(m * 2 * CW, 2 * CW))
+        return local(wd_h.at[sl], wd.at[sl], L_DN + m)
 
     for c in first + cp_wq + cp_k:
         c.start()
@@ -135,19 +139,22 @@
     sinv = jnp.sin(angles) * ROPE_MSCALE
     low_half = (lane48 % HD) < (HD // 2)
 
-    def rope(x):
+    def rope(x, both=False):
         xf = x.astype(BF16).astype(F32)
-        rot = jnp.where(low_half, -pltpu.roll(xf, 96, 1), pltpu.roll(xf, 32, 1))
-        return (xf * cosv + rot * sinv).astype(BF16).astype(F32)
+        up, down_ = pltpu.roll(xf, 96, 1), pltpu.roll(xf, 32, 1)
+        plain = (xf * cosv + jnp.where(low_half, -up, down_) * sinv).astype(BF16).astype(F32)
+        if not both:
+            return plain
+        return plain, (pltpu.roll(xf, HD, 1) * cosv + jnp.where(low_half, -down_, up) * sinv).astype(BF16).astype(F32)
 
     h1 = norm_rows(xb[...].reshape(R, D).astype(F32), g1[...], b1[...])
 
     left = lane48 < HD
 
     def put_q(q, p):
-        qa = rope(q[:, :128]) * 0.125
-        qb_ = rope(q[:, 128:]) * 0.125
-        pair = (jnp.where(left, qa, pltpu.roll(qb_, 64, 1)), jnp.where(left, pltpu.roll(qa, 64, 1), qb_))
+        qa, qa_x = rope(q[:, :LN], True)
+        qb, qb_x = rope(q[:, LN:], True)
+        pair = (jnp.where(left, qa, qb_x) * 0.125, jnp.where(left, qa_x, qb) * 0.125)
         for g in range(2):
             for s in range(S):
                 qbuf[:, 2 * s + g, at(p)] = pair[g][at(s, B)]
@@ -238,7 +245,9 @@
     send_o[0].start()
     cp_v[1].wait()
     for i in range(GROUPS):
-        up_copy(wd_h, wd, i, L_DN).start()
+        down_copy(0, i * 4, 4).start()
+    for i in range(GROUPS):
+        down_copy(1, i * 4, 4).start()
     for i in range(8):
         values(1 - core, i, 1)
     for i in range(4):
@@ -307,6 +316,9 @@
     eye = jnp.where(lax.broadcasted_iota(jnp.int32, (B, B), 0) == lane_iota((B, B)), 1.0, 0.0)
     picks[...] = jnp.concatenate([mm_t(eye, idx[s].astype(F32)) for s in range(S)], axis=0)
 
+    eye_e = jnp.where(lax.broadcasted_iota(jnp.int32, (E, E), 0) == lane_iota((E, E)), 1.0, 0.0).astype(BF16)
+    wrt[...] = lax.dot_general(wr[...], eye_e, (((0,), (0,)), ((), ())), preferred_element_type=F32).astype(BF16)
+
     for c in send_ml[1:]:
         c.wait_recv()
     ml = [mlall[d] for d in range(4)]
@@ -344,23 +356,27 @@
             oall[core, hh, j] = c2[hh, 0, j] * ga[j][:, ln] + c2[hh, 1, j] * gb[j][:, ln] + tl[j][:, ln]
         send_g[hh].start()
 
-    local(wo, wo, L_WO).wait()
-    att = None
-    for hh in range(2):
-        send_g[hh].wait_recv()
-        for g in range(2):
-            o_g = jnp.concatenate([oall[h, hh, 2 * s + g] for s in range(S) for h in range(2)], axis=0).astype(BF16)
-            part = mm(o_g, wo[g, at(hh, T)])
-            att = part if att is None else att + part
-    xm = (xb[...].reshape(R, D).astype(F32) + att + bo[...]).astype(BF16).astype(F32)
-    for n in range(NCH):
-        xm4[n] = xm[:, at(n, CW)]
-    h2 = norm_rows(xm, g2[...], b2[...])
+    here = me < 4
+
+    @pl.when(here)
+    def _():
+        local(wo, wo, L_WO).wait()
+        att = None
+        for hh in range(2):
+            send_g[hh].wait_recv()
+            for g in range(2):
+                o_g = jnp.concatenate([oall[h, hh, 2 * s + g] for s in range(S) for h in range(2)], axis=0).astype(BF16)
+                part = mm(o_g, wo[g, at(hh, T)])
+                att = part if att is None else att + part
+        xm = (xb[...].reshape(R, D).astype(F32) + att + bo[...]).astype(BF16).astype(F32)
+        for n in range(NCH):
+            xm4[n] = xm[:, at(n, CW)]
+        h2[...] = norm_rows(xm, g2[...], b2[...])
 
     def act(i):
         for n in range(4):
             e = i * 4 + n
-            raw[e] = mm(h2, jnp.concatenate([wg[e], wu[e]], axis=1))
+            raw[e] = mm(h2[...], jnp.concatenate([wg[e], wu[e]], axis=1))
 
     def mix(i):
         for n in range(4):
@@ -370,24 +386,25 @@
 
     local(wg, wg, L_GU).wait()
     local(wu, wu, L_GU + 1).wait()
-    logits = mm_t(h2, wr[...])
-    for i in range(4):
-        act(i)
-    lane_e = lane_iota((R, E)).astype(F32)
-    chosen = picks[...]
-    gates = jnp.zeros((R, E), F32)
-    for k in range(8):
-        on = jnp.concatenate([rm[s, :, k, :] for s in range(S)], axis=0) == 1
-        mk = jnp.where(on, logits, NEG_FILL)
-        pk = jnp.exp(mk - jnp.max(mk, axis=1, keepdims=True))
-        pk = pk / jnp.sum(pk, axis=1, keepdims=True)
-        gates = gates + jnp.where(chosen[:, k:k + 1] == lane_e, pk, 0.0)
-    for e in range(E):
-        gx[e] = jnp.broadcast_to(gates[:, e:e + 1], (R, 128))
-
-    for i in range(4, 6):
-        act(i)
-        mix(i - 4)
+
+    @pl.when(here)
+    def _():
+        logits = mm(h2[...], wrt[...])
+        for i in range(4):
+            act(i)
+        lane_e = lane_iota((R, E)).astype(F32)
+        chosen = picks[...]
+        gates = jnp.zeros((R, E), F32)
+        for k in range(8):
+            on = jnp.concatenate([rm[s, :, k, :] for s in range(S)], axis=0) == 1
+            mk = jnp.where(on, logits, NEG_FILL)
+            pk = jnp.exp(mk - jnp.max(mk, axis=1, keepdims=True))
+            pk = pk / jnp.sum(pk, axis=1, keepdims=True)
+            gates = gates + jnp.where(chosen[:, k:k + 1] == lane_e, pk, 0.0)
+        for e in range(E):
+            gx[e] = jnp.broadcast_to(gates[:, e:e + 1], (R, 128))
+
+        act(4)
 
     def down(m):
         u = jnp.concatenate([ub[e] for e in range(E)], axis=1)
@@ -397,30 +414,47 @@
 
     send_a = [remote(pb.at[n], ab.at[n], S_P, R_P + n, partner) for n in range(NCH)]
     send_b = [remote(s2.at[n, chip], s2.at[n, chip], S_B, R_B + n, peer) for n in range(NCH)]
+    send_d = [remote(pb.at[0], db.at[0], S_B, R_B + NCH, diag), remote(pb.at[0], db.at[1], S_B, R_B, peer)]
     send_y = [remote(yb.at[n], yb.at[n], S_P, R_P + n, partner) for n in range(NCH)]
 
-    local(wd, wd, L_DN).wait()
-    for i in range(6, 8):
-        act(i)
-        mix(i - 4)
-    for i in range(4, 8):
-        mix(i)
     for m in range(2):
-        down(m)
+        down_copy(m, 0, E).wait()
+
+        @pl.when(here)
+        def _():
+            if m == 0:
+                for i in range(5, 8):
+                    act(i)
+                    mix(i - 5)
+                for i in range(3, 8):
+                    mix(i)
+            down(m)
 
         @pl.when(core == 0)
         def _():
             for n in (2 * m, 2 * m + 1):
                 send_a[n].start()
+            if m == 0:
+                send_d[0].start()
+
+        if m == 0:
+            @pl.when(core == 1)
+            def _():
+                send_d[1].start()
 
     @pl.when(core == 1)
     def _():
         for n in range(NCH):
             send_a[n].wait_recv()
             s2[n, chip] = ab[n] + pb[n]
-            send_b[n].start()
+            if n > 0:
+                send_b[n].start()
+        for c in send_d:
+            c.wait_recv()
+        s2[0, 1 - chip] = db[0] + db[1]
         for n in range(NCH):
-            send_b[n].wait_recv()
+            if n > 0:
+                send_b[n].wait_recv()
             yb[n] = xm4[n] + (s2[n, 0] + s2[n, 1])
             send_y[n].start()
             hb[:, :, at(n, CW)] = yb[n].astype(BF16).reshape(S, B, CW)
@@ -428,6 +462,7 @@
 
     @pl.when(core == 0)
     def _():
+        send_d[0].wait_send()
         for n in range(NCH):
             send_y[n].wait_recv()
             hb[:, :, at(n, CW)] = yb[n].astype(BF16).reshape(S, B, CW)
@@ -465,8 +500,8 @@
             V((B, 8, 512), F32), V((S, B, 512), F32), V((S, B, 512), F32), V((B, 2, 32, T), F32), V((B, 2, 32, T), BF16),
             V((2, 8, 128), F32), V((4, 8, 128), F32), V((2, 2, 8, 8, 256), F32), V((2, 8, 8, 256), F32), V((2, 2, 8, 8, 256), F32),
             V((4, 8, 8, 512), F32), V((6, 8, 512), F32), V((6, 8, 512), F32), V((6, 8, 512), F32), V((2, 2, 6, 8, 256), F32),
-            V((NCH, R, CW), F32), V((E, R, 128), F32), V((E, R, 2 * FS), F32), V((R, 512), F32), V((R, 8), F32), V((E, R, FS), BF16), V((NCH, R, CW), F32),
-            V((NCH, R, CW), F32), V((NCH, 2, R, CW), F32), V((NCH, R, CW), F32), V((B, S, KV, HD), F32), V((B, S, KV, HD), F32),
+            V((NCH, R, CW), F32), V((E, R, 128), F32), V((E, R, 2 * FS), F32), V((R, 512), F32), V((R, 8), F32), V((D, E), BF16), V((R, D), BF16), V((E, R, FS), BF16), V((NCH, R, CW), F32),
+            V((NCH, R, CW), F32), V((2, R, CW), F32), V((NCH, 2, R, CW), F32), V((NCH, R, CW), F32), V((B, S, KV, HD), F32), V((B, S, KV, HD), F32),
             pltpu.SemaphoreType.DMA((NLOCAL,)), pltpu.SemaphoreType.DMA((NSEND,)), pltpu.SemaphoreType.DMA((NRECV,)),
         ]
         anyspec = pl.BlockSpec(memory_space=pl.ANY)

time: 24.4 us -> 23.9 us (0.980)
  Pallas kernels: 23.6 us -> 23.2 us
    pallas_call x1, Pallas kernels: 22.9 us -> 22.5 us  [layer_steps(): pl.pallas_call(kernel, out_shape=tuple((V(*o) for o in outs)), in_specs=[...]
where the time goes in v5:
time: 23.9 us; the launch traced here: 23.8 us
  Pallas kernels  23.2 us (97%)
  between operations  0.65 us (3%)
    pallas_call x1, Pallas kernels, layer_steps(): pl.pallas_call(kernel, out_shape=tuple((V(*o) for o in outs)), in_specs=[...  22.5 us
    pallas_call x1, Pallas kernels, layer_steps(): pl.pallas_call(write_kernel, out_shape=tuple((jax.ShapeDtypeStruct(*o) fo...  0.73 us

profile of v5, /device:TPU:0, one launch (start us, length us, event | category | flops | bytes accessed | tf_op | source)
XLA Modules:
  0.0 23.8 jit_solution(16651467034688096960)
XLA Ops:
  0.6 22.5 %shard_map.256 = (bf16[3,16,1024]{2,1,0:T(8,128)(2,1)S(1)}, bf16[16,3,8,64]{3,2,1,0:T(8,128)(2,1)S(1)}, bf16[16,3,8,64]{3,2,1,0:T(8,128)(2,1)S(1)}) custom-call(bf16[16,1024]{1,0:T(8,128)(2,1)} %x_first.1, bf16[2,16,1024]{2,1,0:T(8,128)(2,1)} %next_emb.1, bf16[16,8,64,256]{3,2,1,0:T(8,128)(2,1)} %bitcast.13, bf16[16,8,64,256]{3,2,1,0:T(8,128)(2,1)} %bitcast.14, ...), custom_call_target="tpu_custom_call" | custom-call | tf_op jit(solution)/shard_map/pallas_call | solution.py:510
  23.1 0.7 %shard_map.257 = (bf16[3,16,1024]{2,1,0:T(8,128)(2,1)}, bf16[16,3,8,64]{3,2,1,0:T(8,128)(2,1)}, bf16[16,3,8,64]{3,2,1,0:T(8,128)(2,1)}) custom-call(bf16[3,16,1024]{2,1,0:T(8,128)(2,1)S(1)} %get-tuple-element.6.h, bf16[16,3,8,64]{3,2,1,0:T(8,128)(2,1)S(1)} %get-tuple-element.7.tk, bf16[16,3,8,64]{3,2,1,0:T(8,128)(2,1)S(1)} %get-tuple-element.8.tv), custom_call_target="tpu_custom_call" | custom-call | tf_op jit(solution)/shard_map/pallas_call | solution.py:518

commit v6 on v5

--- a/solution.py
+++ b/solution.py
@@ -31,11 +31,11 @@
 
 GROUPS = 8
 SMALL, PARTS = 8, 4
-L_SMALL, L_WQ, L_K, L_V, L_WO, L_GU, L_DN, NLOCAL = itertools.accumulate((SMALL, 2, PARTS, PARTS, 1, 2, 2), initial=0)
+L_SMALL, L_WQ, L_K, L_V, L_WO, L_GU, L_DN, NLOCAL = itertools.accumulate((SMALL, 2, PARTS, PARTS, 1, PARTS, 2), initial=0)
 R_ML, R_O, R_C, R_G, R_P, R_B, NRECV = itertools.accumulate((3, 2, 2, 2, NCH, NCH + 1), initial=0)
 S_ML, S_O, S_C, S_G, S_P, S_B, NSEND = range(7)
 LN = 128
-HALF = 8
+TWO, FOUR, EIGHT = range(2), range(4), range(8)
 
 
 def at(i, width=LN):
@@ -66,7 +66,7 @@
     wr_h, wg_h, wu_h, wd_h, lf_h, idx_h, rm_h, base_h,
     hb, tkb, tvb,
     xb, g1, b1, wq, bq, wk, bk, wv, bv, wo, bo, g2, b2, wr, wg, wu, wd, lf, idx, rm, base, seq_s, kc, vc,
-    qbuf, kbuf, vbuf, sbuf, wbuf, mlb, mlall, obuf, orecv, c2, ex, ga, gb, tl, oall, xm4, gx, raw, qraw, picks, wrt, h2, ub, pb, ab, db, s2, yb, tkf, tvf,
+    qbuf, kbuf, vbuf, sbuf, wbuf, mlb, mlall, obuf, orecv, c2, ex, ga, gb, tl, oall, xm4, gx, raw, qraw, dsum, picks, wrt, h2, ub, pb, ab, db, s2, yb, tkf, tvf,
     lsem, ssem, rsem,
 ):
     me = lax.axis_index("kv")
@@ -90,7 +90,7 @@
             (seq_hbm, seq_s), (bk_h, bk), (bv_h, bv), (bo_h, bo), (g2_h, g2), (b2_h, b2), (wr_h, wr), (idx_h, idx), (rm_h, rm)))
     ]
     first, later = small[:SMALL], small[SMALL:]
-    cp_wq = [local(wq_h.at[:, pl.ds(i * 512, 512)], wq.at[:, pl.ds(i * 512, 512)], L_WQ + i) for i in range(2)]
+    cp_wq = [local(wq_h.at[:, pl.ds(i * 512, 512)], wq.at[:, pl.ds(i * 512, 512)], L_WQ + i) for i in TWO]
     other, own = (1 - core) * 8, core * 8
 
     def k_part(i):
@@ -101,11 +101,11 @@
         sl = (pl.ds(other if i < 2 else own, 8), pl.ds((i % 2) * 4, 4))
         return local(v_hbm.at[sl], vc.at[sl], L_V + i)
 
-    cp_k = [k_part(i) for i in range(4)]
-    cp_v = [v_part(i) for i in range(4)]
+    cp_k = [k_part(i) for i in FOUR]
+    cp_v = [v_part(i) for i in FOUR]
     cp_wkv = [local(wk_h, wk, L_WQ), local(wv_h, wv, L_WQ + 1)]
     cp_wo = [
-        local(wo_h.at[pl.ds(kv * 128 + g * 64, 64)], wo.at[g, pl.ds(kv * 64, 64)], L_WO) for kv in range(KV) for g in range(2)
+        local(wo_h.at[pl.ds(kv * 128 + g * 64, 64)], wo.at[g, pl.ds(kv * 64, 64)], L_WO) for kv in range(KV) for g in TWO
     ]
 
     def up_copy(src, dst, i, sem):
@@ -116,7 +116,7 @@
         sl = (pl.ds(e, n), pl.ds(0, FS), pl.ds(m * 2 * CW, 2 * CW))
         return local(wd_h.at[sl], wd.at[sl], L_DN + m)
 
-    for c in first + cp_wq + cp_k:
+    for c in first + cp_wq + cp_k[:3] + cp_v[:1] + cp_k[3:]:
         c.start()
     bar = pltpu.get_barrier_semaphore()
     for dev in (partner, peer, diag):
@@ -125,7 +125,7 @@
 
     for c in first:
         c.wait()
-    for c in cp_v:
+    for c in cp_v[1:]:
         c.start()
 
     lane48 = lane_iota((R, 128))
@@ -155,7 +155,7 @@
         qa, qa_x = rope(q[:, :LN], True)
         qb, qb_x = rope(q[:, LN:], True)
         pair = (jnp.where(left, qa, qb_x) * 0.125, jnp.where(left, qa_x, qb) * 0.125)
-        for g in range(2):
+        for g in TWO:
             for s in range(S):
                 qbuf[:, 2 * s + g, at(p)] = pair[g][at(s, B)]
 
@@ -166,7 +166,7 @@
     for c in later + cp_wo + cp_wkv:
         c.start()
     q_hi = mm(h1, wq[:, 512:]) + bq[:, 512:]
-    for p in range(4):
+    for p in FOUR:
         put_q(qraw[:, p * 256:(p + 1) * 256] if p < 2 else q_hi[:, (p - 2) * 256:(p - 1) * 256], p)
 
     rowq = lax.broadcasted_iota(jnp.int32, (32, T), 0)
@@ -177,20 +177,20 @@
 
     def scores(start, i):
         qv = qbuf[start + i]
-        for hh in range(2):
+        for hh in TWO:
             rep = jnp.concatenate([qv[:, at(hh, T)]] * 4, axis=0)
             lhs = jnp.where(diag_mask, rep, 0.0).astype(BF16)
             sbuf[start + i, hh] = mm(lhs, kc[start + i, at(hh, 4)].reshape(256, T))
 
     def soft(start, i, acc):
         keep = pos < seq_s[start + i]
-        for hh in range(2):
+        for hh in TWO:
             sc = jnp.where(keep, sbuf[start + i, hh], NEG_FILL)
             m = jnp.max(sc, axis=1, keepdims=True)
             w = jnp.where(keep, jnp.exp(sc - m), 0.0)
             l = jnp.sum(w, axis=1, keepdims=True)
             wbuf[start + i, hh] = w.astype(BF16)
-            for j in range(4):
+            for j in FOUR:
                 spot = i * 16 + hh * 4 + j
                 acc = jnp.where(lane8 == spot, m[at(j, 8)], acc)
                 acc = jnp.where(lane8 == spot + 8, l[at(j, 8)], acc)
@@ -208,25 +208,26 @@
         remote(mlb.at[1 - core], mlall.at[me], S_ML, R_ML, partner), remote(mlb.at[core], mlall.at[me], S_ML, R_ML + 1, peer),
         remote(mlb.at[1 - core], mlall.at[me], S_ML, R_ML + 2, diag),
     ]
-    send_o = [remote(obuf.at[1 - core, hh], orecv.at[hh], S_O, R_O + hh, partner) for hh in range(2)]
+    send_o = [remote(obuf.at[1 - core, hh], orecv.at[hh], S_O, R_O + hh, partner) for hh in TWO]
     zero = jnp.zeros((8, 128), F32)
 
     cp_k[0].wait()
-    for i in range(4):
+    for i in FOUR:
         scores(other, i)
     cp_k[1].wait()
-    for i in range(4):
+    for i in FOUR:
         scores(other, 4 + i)
     acc = zero
-    for i in range(4):
+    for i in FOUR:
         acc = soft(other, i, acc)
     cp_k[2].wait()
     for i in range(GROUPS):
-        up_copy(wg_h, wg, i, L_GU).start()
-        up_copy(wu_h, wu, i, L_GU + 1).start()
-    for i in range(4):
+        sem = L_GU + 2 * (i // 5)
+        up_copy(wg_h, wg, i, sem).start()
+        up_copy(wu_h, wu, i, sem + 1).start()
+    for i in FOUR:
         scores(own, i)
-    for i in range(4):
+    for i in FOUR:
         acc = soft(other, 4 + i, acc)
     mlb[1 - core] = acc
     pl.semaphore_wait(bar, 3)
@@ -234,27 +235,30 @@
     send_ml[2].start()
 
     cp_v[0].wait()
-    cp_k[3].wait()
-    for i in range(8):
+    for i in EIGHT:
         values(1 - core, i, 0)
-    for i in range(4):
-        scores(own, 4 + i)
     acc = zero
-    for i in range(4):
+    for i in FOUR:
         acc = soft(own, i, acc)
     send_o[0].start()
     cp_v[1].wait()
+    cp_k[3].wait()
     for i in range(GROUPS):
         down_copy(0, i * 4, 4).start()
     for i in range(GROUPS):
         down_copy(1, i * 4, 4).start()
-    for i in range(8):
+    for i in EIGHT:
         values(1 - core, i, 1)
-    for i in range(4):
+    for i in FOUR:
+        scores(own, 4 + i)
+    send_o[1].start()
+    cp_v[2].wait()
+    for i in FOUR:
         acc = soft(own, 4 + i, acc)
     mlb[core] = acc
     mlall[me] = acc
-    send_o[1].start()
+    for i in EIGHT:
+        values(core, i, 0)
     send_ml[1].start()
 
     pick = (lane8 // HD)
@@ -262,12 +266,13 @@
     def spread(v, i, p):
         return jnp.take_along_axis(v, pick + (i * 16 + 2 * p), axis=1, mode="promise_in_bounds")
 
-    send_c = [remote(c2.at[hh, chip, pl.ds(0, 6)], c2.at[hh, chip, pl.ds(0, 6)], S_C, R_C + hh, peer) for hh in range(2)]
-    for hh in range(2):
-        cp_v[2 + hh].wait()
-        for i in range(8):
-            values(core, i, hh)
-        if hh == 0:
+    send_c = [remote(c2.at[hh, chip, pl.ds(0, 6)], c2.at[hh, chip, pl.ds(0, 6)], S_C, R_C + hh, peer) for hh in TWO]
+    for hh in TWO:
+        if hh == 1:
+            cp_v[3].wait()
+            for i in EIGHT:
+                values(core, i, 1)
+        else:
             send_ml[0].wait_recv()
             ml_a = mlall[me]
             ml_b = mlall[partner]
@@ -275,10 +280,10 @@
             f_a = jnp.exp(ml_a - m_ab)
             f_b = jnp.exp(ml_b - m_ab)
         send_o[hh].wait_recv()
-        for i in range(8):
+        for i in EIGHT:
             oa = obuf[core, hh, i]
             ob = orecv[hh, i]
-            for p in range(2):
+            for p in TWO:
                 ln = at(p)
                 c2[hh, chip, :, i, ln] = (
                     oa[:, ln] * spread(f_a, i, 2 * hh + p) + ob[:, ln] * spread(f_b, i, 2 * hh + p))
@@ -289,7 +294,7 @@
     kn = mm(h1, wk[...]) + bk[...]
     vn = (mm(h1, wv[...]) + bv[...]).astype(BF16)
     vn = vn.astype(F32)
-    for p in range(4):
+    for p in FOUR:
         ln = at(p)
         for val, buf, fin in ((rope(kn[:, ln]), kbuf, tkf), (vn[:, ln], vbuf, tvf)):
             swap = pltpu.roll(val, 64, 1)
@@ -304,14 +309,14 @@
     rows = pl.ds(pl.multiple_of(core * 8, 8), 8)
     kt = [kbuf[t, rows, :] for t in range(S)]
     vt = [vbuf[t, rows, :] for t in range(S)]
-    trip = [(s, g, t) for s in range(S) for g in range(2) for t in range(s + 1)]
+    trip = [(s, g, t) for s in range(S) for g in TWO for t in range(s + 1)]
     prod = jnp.concatenate([qbuf[rows, 2 * s + g, :] * kt[t] for s, g, t in trip], axis=0)
     hi = prod.astype(BF16)
     lo = (prod - hi.astype(F32)).astype(BF16)
     r2 = lax.broadcasted_iota(jnp.int32, (256, 128), 0)
     ones = jnp.where(((r2 % 128) // HD) == (lane_iota((256, 128)) // HD), 1.0, 0.0).astype(BF16)
     tsc = jnp.concatenate(
-        [mm(jnp.concatenate([hi[:, at(p)], lo[:, at(p)]], axis=1), ones) for p in range(4)], axis=1)
+        [mm(jnp.concatenate([hi[:, at(p)], lo[:, at(p)]], axis=1), ones) for p in FOUR], axis=1)
 
     eye = jnp.where(lax.broadcasted_iota(jnp.int32, (B, B), 0) == lane_iota((B, B)), 1.0, 0.0)
     picks[...] = jnp.concatenate([mm_t(eye, idx[s].astype(F32)) for s in range(S)], axis=0)
@@ -321,19 +326,19 @@
 
     for c in send_ml[1:]:
         c.wait_recv()
-    ml = [mlall[d] for d in range(4)]
-    for ch in range(2):
+    ml = [mlall[d] for d in FOUR]
+    for ch in TWO:
         a, b_ = ml[2 * ch], ml[2 * ch + 1]
         mc = jnp.maximum(a, b_)
         lc = (pltpu.roll(a, 120, 1) * jnp.exp(a - mc) + pltpu.roll(b_, 120, 1) * jnp.exp(b_ - mc))
-        for i in range(8):
-            for p in range(4):
+        for i in EIGHT:
+            for p in FOUR:
                 ln = at(p)
                 ex[2 * ch, :, i, ln] = spread(mc, i, p)
                 ex[2 * ch + 1, :, i, ln] = spread(lc, i, p)
 
     for s in range(S):
-        for g in range(2):
+        for g in TWO:
             j = 2 * s + g
             sc = [tsc[at(n, 8)] for n, key in enumerate(trip) if key[:2] == (s, g)]
             mt = functools.reduce(jnp.maximum, sc)
@@ -348,8 +353,8 @@
             gb[j] = f1 * inv_l
             tl[j] = ot * (ft * inv_l)
 
-    send_g = [remote(oall.at[core, hh], oall.at[core, hh], S_G, R_G + hh, partner) for hh in range(2)]
-    for hh in range(2):
+    send_g = [remote(oall.at[core, hh], oall.at[core, hh], S_G, R_G + hh, partner) for hh in TWO]
+    for hh in TWO:
         send_c[hh].wait_recv()
         ln = at(hh, T)
         for j in range(6):
@@ -362,10 +367,10 @@
     def _():
         local(wo, wo, L_WO).wait()
         att = None
-        for hh in range(2):
+        for hh in TWO:
             send_g[hh].wait_recv()
-            for g in range(2):
-                o_g = jnp.concatenate([oall[h, hh, 2 * s + g] for s in range(S) for h in range(2)], axis=0).astype(BF16)
+            for g in TWO:
+                o_g = jnp.concatenate([oall[h, hh, 2 * s + g] for s in range(S) for h in TWO], axis=0).astype(BF16)
                 part = mm(o_g, wo[g, at(hh, T)])
                 att = part if att is None else att + part
         xm = (xb[...].reshape(R, D).astype(F32) + att + bo[...]).astype(BF16).astype(F32)
@@ -374,28 +379,31 @@
         h2[...] = norm_rows(xm, g2[...], b2[...])
 
     def act(i):
-        for n in range(4):
+        for n in FOUR:
             e = i * 4 + n
             raw[e] = mm(h2[...], jnp.concatenate([wg[e], wu[e]], axis=1))
 
     def mix(i):
-        for n in range(4):
+        for n in FOUR:
             e = i * 4 + n
             a, up = raw[e, :, :FS], raw[e, :, FS:]
             ub[e] = (gx[e] * (a * (1.0 / (1.0 + jnp.exp(-a)))) * up).astype(BF16)
 
-    local(wg, wg, L_GU).wait()
-    local(wu, wu, L_GU + 1).wait()
+    def wait_up(sl, sem):
+        for n, w in enumerate((wg, wu)):
+            local(w.at[sl], w.at[sl], sem + n).wait()
+
+    wait_up(pl.ds(0, 20), L_GU)
 
     @pl.when(here)
     def _():
         logits = mm(h2[...], wrt[...])
-        for i in range(4):
+        for i in FOUR:
             act(i)
         lane_e = lane_iota((R, E)).astype(F32)
         chosen = picks[...]
         gates = jnp.zeros((R, E), F32)
-        for k in range(8):
+        for k in EIGHT:
             on = jnp.concatenate([rm[s, :, k, :] for s in range(S)], axis=0) == 1
             mk = jnp.where(on, logits, NEG_FILL)
             pk = jnp.exp(mk - jnp.max(mk, axis=1, keepdims=True))
@@ -406,19 +414,22 @@
 
         act(4)
 
-    def down(m):
-        u = jnp.concatenate([ub[e] for e in range(E)], axis=1)
-        part = mm(u, wd[:, :, at(m, 2 * CW)].reshape(E * FS, 2 * CW)).astype(BF16).astype(F32)
-        pb[2 * m] = part[:, :CW]
-        pb[2 * m + 1] = part[:, CW:]
+    def down(n, first, count, width):
+        u = jnp.concatenate([ub[e] for e in range(first, first + count)], axis=1)
+        return mm(u, wd[first:first + count, :, n * CW:n * CW + width].reshape(count * FS, width))
+
+    def rounded(x):
+        return x.astype(BF16).astype(F32)
 
     send_a = [remote(pb.at[n], ab.at[n], S_P, R_P + n, partner) for n in range(NCH)]
     send_b = [remote(s2.at[n, chip], s2.at[n, chip], S_B, R_B + n, peer) for n in range(NCH)]
     send_d = [remote(pb.at[0], db.at[0], S_B, R_B + NCH, diag), remote(pb.at[0], db.at[1], S_B, R_B, peer)]
     send_y = [remote(yb.at[n], yb.at[n], S_P, R_P + n, partner) for n in range(NCH)]
 
-    for m in range(2):
-        down_copy(m, 0, E).wait()
+    wait_up(pl.ds(20, 12), L_GU + 2)
+    for m in range(3):
+        if m < 2:
+            down_copy(m, 0, E).wait()
 
         @pl.when(here)
         def _():
@@ -428,11 +439,17 @@
                     mix(i - 5)
                 for i in range(3, 8):
                     mix(i)
-            down(m)
+                part = rounded(down(0, 0, E, 2 * CW))
+                pb[0] = part[:, :CW]
+                pb[1] = part[:, CW:]
+            else:
+                for h in TWO:
+                    dsum[h] = down(m + 1, h * (E // 2), E // 2, CW)
+                pb[m + 1] = rounded(dsum[0] + dsum[1])
 
         @pl.when(core == 0)
         def _():
-            for n in (2 * m, 2 * m + 1):
+            for n in ((0, 1) if m == 0 else (m + 1,)):
                 send_a[n].start()
             if m == 0:
                 send_d[0].start()
@@ -500,7 +517,7 @@
             V((B, 8, 512), F32), V((S, B, 512), F32), V((S, B, 512), F32), V((B, 2, 32, T), F32), V((B, 2, 32, T), BF16),
             V((2, 8, 128), F32), V((4, 8, 128), F32), V((2, 2, 8, 8, 256), F32), V((2, 8, 8, 256), F32), V((2, 2, 8, 8, 256), F32),
             V((4, 8, 8, 512), F32), V((6, 8, 512), F32), V((6, 8, 512), F32), V((6, 8, 512), F32), V((2, 2, 6, 8, 256), F32),
-            V((NCH, R, CW), F32), V((E, R, 128), F32), V((E, R, 2 * FS), F32), V((R, 512), F32), V((R, 8), F32), V((D, E), BF16), V((R, D), BF16), V((E, R, FS), BF16), V((NCH, R, CW), F32),
+            V((NCH, R, CW), F32), V((E, R, 128), F32), V((E, R, 2 * FS), F32), V((R, 512), F32), V((2, R, CW), F32), V((R, 8), F32), V((D, E), BF16), V((R, D), BF16), V((E, R, FS), BF16), V((NCH, R, CW), F32),
             V((NCH, R, CW), F32), V((2, R, CW), F32), V((NCH, 2, R, CW), F32), V((NCH, R, CW), F32), V((B, S, KV, HD), F32), V((B, S, KV, HD), F32),
             pltpu.SemaphoreType.DMA((NLOCAL,)), pltpu.SemaphoreType.DMA((NSEND,)), pltpu.SemaphoreType.DMA((NRECV,)),
         ]

time: 23.9 us -> 23 us (0.962)
  Pallas kernels: 23.2 us -> 22.2 us
    pallas_call x1, Pallas kernels: 22.5 us -> 21.5 us  [layer_steps(): pl.pallas_call(kernel, out_shape=tuple((V(*o) for o in outs)), in_specs=[...]
where the time goes in v6:
time: 23 us; the launch traced here: 22.9 us
  Pallas kernels  22.2 us (97%)
  between operations  0.65 us (3%)
    pallas_call x1, Pallas kernels, layer_steps(): pl.pallas_call(kernel, out_shape=tuple((V(*o) for o in outs)), in_specs=[...  21.5 us
    pallas_call x1, Pallas kernels, layer_steps(): pl.pallas_call(write_kernel, out_shape=tuple((jax.ShapeDtypeStruct(*o) fo...  0.73 us

profile of v6, /device:TPU:0, one launch (start us, length us, event | category | flops | bytes accessed | tf_op | source)
XLA Modules:
  0.0 22.9 jit_solution(1133819705838326038)
XLA Ops:
  0.6 21.5 %shard_map.256 = (bf16[3,16,1024]{2,1,0:T(8,128)(2,1)S(1)}, bf16[16,3,8,64]{3,2,1,0:T(8,128)(2,1)S(1)}, bf16[16,3,8,64]{3,2,1,0:T(8,128)(2,1)S(1)}) custom-call(bf16[16,1024]{1,0:T(8,128)(2,1)} %x_first.1, bf16[2,16,1024]{2,1,0:T(8,128)(2,1)} %next_emb.1, bf16[16,8,64,256]{3,2,1,0:T(8,128)(2,1)} %bitcast.13, bf16[16,8,64,256]{3,2,1,0:T(8,128)(2,1)} %bitcast.14, ...), custom_call_target="tpu_custom_call" | custom-call | tf_op jit(solution)/shard_map/pallas_call | solution.py:527
  22.2 0.7 %shard_map.257 = (bf16[3,16,1024]{2,1,0:T(8,128)(2,1)}, bf16[16,3,8,64]{3,2,1,0:T(8,128)(2,1)}, bf16[16,3,8,64]{3,2,1,0:T(8,128)(2,1)}) custom-call(bf16[3,16,1024]{2,1,0:T(8,128)(2,1)S(1)} %get-tuple-element.6.h, bf16[16,3,8,64]{3,2,1,0:T(8,128)(2,1)S(1)} %get-tuple-element.7.tk, bf16[16,3,8,64]{3,2,1,0:T(8,128)(2,1)S(1)} %get-tuple-element.8.tv), custom_call_target="tpu_custom_call" | custom-call | tf_op jit(solution)/shard_map/pallas_call | solution.py:535

commit v7 on v6

--- a/solution.py
+++ b/solution.py
@@ -291,20 +291,25 @@
 
     for c in later + cp_wkv:
         c.wait()
+    for c in send_ml[1:]:
+        c.wait_recv()
     kn = mm(h1, wk[...]) + bk[...]
     vn = (mm(h1, wv[...]) + bv[...]).astype(BF16)
     vn = vn.astype(F32)
     for p in FOUR:
         ln = at(p)
-        for val, buf, fin in ((rope(kn[:, ln]), kbuf, tkf), (vn[:, ln], vbuf, tvf)):
-            swap = pltpu.roll(val, 64, 1)
+        for val, buf in ((rope(kn[:, ln]), kbuf), (vn[:, ln], vbuf)):
             for s in range(S):
-                r = at(s, B)
-                buf[s, :, ln] = val[r]
-                fin[:, s, 2 * p, :] = val[r, :HD]
-                fin[:, s, 2 * p + 1, :] = swap[r, :HD]
-    tkb[...] = tkf[...].astype(BF16)
-    tvb[...] = tvf[...].astype(BF16)
+                buf[s, :, ln] = val[at(s, B)]
+
+    def tails():
+        for buf, fin, out in ((kbuf, tkf, tkb), (vbuf, tvf, tvb)):
+            for p in FOUR:
+                for s in range(S):
+                    val = buf[s, :, at(p)]
+                    fin[:, s, 2 * p, :] = val[:, :HD]
+                    fin[:, s, 2 * p + 1, :] = pltpu.roll(val, HD, 1)[:, :HD]
+            out[...] = fin[...].astype(BF16)
 
     rows = pl.ds(pl.multiple_of(core * 8, 8), 8)
     kt = [kbuf[t, rows, :] for t in range(S)]
@@ -318,14 +323,6 @@
     tsc = jnp.concatenate(
         [mm(jnp.concatenate([hi[:, at(p)], lo[:, at(p)]], axis=1), ones) for p in FOUR], axis=1)
 
-    eye = jnp.where(lax.broadcasted_iota(jnp.int32, (B, B), 0) == lane_iota((B, B)), 1.0, 0.0)
-    picks[...] = jnp.concatenate([mm_t(eye, idx[s].astype(F32)) for s in range(S)], axis=0)
-
-    eye_e = jnp.where(lax.broadcasted_iota(jnp.int32, (E, E), 0) == lane_iota((E, E)), 1.0, 0.0).astype(BF16)
-    wrt[...] = lax.dot_general(wr[...], eye_e, (((0,), (0,)), ((), ())), preferred_element_type=F32).astype(BF16)
-
-    for c in send_ml[1:]:
-        c.wait_recv()
     ml = [mlall[d] for d in FOUR]
     for ch in TWO:
         a, b_ = ml[2 * ch], ml[2 * ch + 1]
@@ -360,6 +357,12 @@
         for j in range(6):
             oall[core, hh, j] = c2[hh, 0, j] * ga[j][:, ln] + c2[hh, 1, j] * gb[j][:, ln] + tl[j][:, ln]
         send_g[hh].start()
+
+    eye = jnp.where(lax.broadcasted_iota(jnp.int32, (B, B), 0) == lane_iota((B, B)), 1.0, 0.0)
+    picks[...] = jnp.concatenate([mm_t(eye, idx[s].astype(F32)) for s in range(S)], axis=0)
+
+    eye_e = jnp.where(lax.broadcasted_iota(jnp.int32, (E, E), 0) == lane_iota((E, E)), 1.0, 0.0).astype(BF16)
+    wrt[...] = lax.dot_general(wr[...], eye_e, (((0,), (0,)), ((), ())), preferred_element_type=F32).astype(BF16)
 
     here = me < 4
 
@@ -427,6 +430,15 @@
     send_y = [remote(yb.at[n], yb.at[n], S_P, R_P + n, partner) for n in range(NCH)]
 
     wait_up(pl.ds(20, 12), L_GU + 2)
+
+    @pl.when(here)
+    def _():
+        for i in range(5, 8):
+            act(i)
+            mix(i - 5)
+        for i in range(3, 7):
+            mix(i)
+
     for m in range(3):
         if m < 2:
             down_copy(m, 0, E).wait()
@@ -434,11 +446,7 @@
         @pl.when(here)
         def _():
             if m == 0:
-                for i in range(5, 8):
-                    act(i)
-                    mix(i - 5)
-                for i in range(3, 8):
-                    mix(i)
+                mix(7)
                 part = rounded(down(0, 0, E, 2 * CW))
                 pb[0] = part[:, :CW]
                 pb[1] = part[:, CW:]
@@ -466,6 +474,7 @@
             s2[n, chip] = ab[n] + pb[n]
             if n > 0:
                 send_b[n].start()
+        tails()
         for c in send_d:
             c.wait_recv()
         s2[0, 1 - chip] = db[0] + db[1]
@@ -479,6 +488,7 @@
 
     @pl.when(core == 0)
     def _():
+        tails()
         send_d[0].wait_send()
         for n in range(NCH):
             send_y[n].wait_recv()

time: 23 us -> 22.4 us (0.974)
  Pallas kernels: 22.2 us -> 21.7 us
    pallas_call x1, Pallas kernels: 21.5 us -> 20.9 us  [layer_steps(): pl.pallas_call(kernel, out_shape=tuple((V(*o) for o in outs)), in_specs=[...]
where the time goes in v7:
time: 22.4 us; the launch traced here: 22.3 us
  Pallas kernels  21.7 us (97%)
  between operations  0.65 us (3%)
    pallas_call x1, Pallas kernels, layer_steps(): pl.pallas_call(kernel, out_shape=tuple((V(*o) for o in outs)), in_specs=[...  20.9 us
    pallas_call x1, Pallas kernels, layer_steps(): pl.pallas_call(write_kernel, out_shape=tuple((jax.ShapeDtypeStruct(*o) fo...  0.73 us

profile of v7, /device:TPU:0, one launch (start us, length us, event | category | flops | bytes accessed | tf_op | source)
XLA Modules:
  0.0 22.3 jit_solution(17620945885519471584)
XLA Ops:
  0.6 20.9 %shard_map.256 = (bf16[3,16,1024]{2,1,0:T(8,128)(2,1)S(1)}, bf16[16,3,8,64]{3,2,1,0:T(8,128)(2,1)S(1)}, bf16[16,3,8,64]{3,2,1,0:T(8,128)(2,1)S(1)}) custom-call(bf16[16,1024]{1,0:T(8,128)(2,1)} %x_first.1, bf16[2,16,1024]{2,1,0:T(8,128)(2,1)} %next_emb.1, bf16[16,8,64,256]{3,2,1,0:T(8,128)(2,1)} %bitcast.13, bf16[16,8,64,256]{3,2,1,0:T(8,128)(2,1)} %bitcast.14, ...), custom_call_target="tpu_custom_call" | custom-call | tf_op jit(solution)/shard_map/pallas_call | solution.py:537
  21.6 0.7 %shard_map.257 = (bf16[3,16,1024]{2,1,0:T(8,128)(2,1)}, bf16[16,3,8,64]{3,2,1,0:T(8,128)(2,1)}, bf16[16,3,8,64]{3,2,1,0:T(8,128)(2,1)}) custom-call(bf16[3,16,1024]{2,1,0:T(8,128)(2,1)S(1)} %get-tuple-element.6.h, bf16[16,3,8,64]{3,2,1,0:T(8,128)(2,1)S(1)} %get-tuple-element.7.tk, bf16[16,3,8,64]{3,2,1,0:T(8,128)(2,1)S(1)} %get-tuple-element.8.tv), custom_call_target="tpu_custom_call" | custom-call | tf_op jit(solution)/shard_map/pallas_call | solution.py:545

commit v8 on v7

--- a/solution.py
+++ b/solution.py
@@ -28,6 +28,7 @@
 R = S * B
 NCH = 4
 CW = D // NCH
+LAST = NCH - 1
 
 GROUPS = 8
 SMALL, PARTS = 8, 4
@@ -241,25 +242,24 @@
     for i in FOUR:
         acc = soft(own, i, acc)
     send_o[0].start()
+    cp_k[3].wait()
+    for i in FOUR:
+        scores(own, 4 + i)
     cp_v[1].wait()
-    cp_k[3].wait()
-    for i in range(GROUPS):
-        down_copy(0, i * 4, 4).start()
-    for i in range(GROUPS):
-        down_copy(1, i * 4, 4).start()
+    for m in TWO:
+        for i in range(GROUPS):
+            down_copy(m, i * 4, 4).start()
     for i in EIGHT:
         values(1 - core, i, 1)
-    for i in FOUR:
-        scores(own, 4 + i)
-    send_o[1].start()
-    cp_v[2].wait()
     for i in FOUR:
         acc = soft(own, 4 + i, acc)
     mlb[core] = acc
     mlall[me] = acc
+    send_o[1].start()
+    send_ml[1].start()
+    cp_v[2].wait()
     for i in EIGHT:
         values(core, i, 0)
-    send_ml[1].start()
 
     pick = (lane8 // HD)
 
@@ -427,6 +427,10 @@
     send_a = [remote(pb.at[n], ab.at[n], S_P, R_P + n, partner) for n in range(NCH)]
     send_b = [remote(s2.at[n, chip], s2.at[n, chip], S_B, R_B + n, peer) for n in range(NCH)]
     send_d = [remote(pb.at[0], db.at[0], S_B, R_B + NCH, diag), remote(pb.at[0], db.at[1], S_B, R_B, peer)]
+    send_last = [
+        remote(s2.at[LAST, chip], s2.at[LAST, chip], S_B, R_B + LAST, diag),
+        remote(s2.at[LAST, chip], s2.at[LAST, chip], S_B, R_B + LAST - 1, partner),
+    ]
     send_y = [remote(yb.at[n], yb.at[n], S_P, R_P + n, partner) for n in range(NCH)]
 
     wait_up(pl.ds(20, 12), L_GU + 2)
@@ -462,18 +466,27 @@
             if m == 0:
                 send_d[0].start()
 
-        if m == 0:
-            @pl.when(core == 1)
-            def _():
+        @pl.when(core == 1)
+        def _():
+            if m == 0:
                 send_d[1].start()
+            for n in ((), (0, 1), (2, LAST))[m]:
+                send_a[n].wait_recv()
+                s2[n, chip] = ab[n] + pb[n]
+                if n == LAST:
+                    for c in send_last:
+                        c.start()
+                if n > 0:
+                    send_b[n].start()
+
+    def finish(n):
+        yb[n] = xm4[n] + (s2[n, 0] + s2[n, 1])
+
+    def put(n):
+        hb[:, :, at(n, CW)] = yb[n].astype(BF16).reshape(S, B, CW)
 
     @pl.when(core == 1)
     def _():
-        for n in range(NCH):
-            send_a[n].wait_recv()
-            s2[n, chip] = ab[n] + pb[n]
-            if n > 0:
-                send_b[n].start()
         tails()
         for c in send_d:
             c.wait_recv()
@@ -481,20 +494,27 @@
         for n in range(NCH):
             if n > 0:
                 send_b[n].wait_recv()
-            yb[n] = xm4[n] + (s2[n, 0] + s2[n, 1])
-            send_y[n].start()
-            hb[:, :, at(n, CW)] = yb[n].astype(BF16).reshape(S, B, CW)
-        remote(s2.at[:, chip], s2.at[:, chip], S_B, R_B, peer).wait_send()
+            finish(n)
+            if n < LAST:
+                send_y[n].start()
+            put(n)
+        for ref, snd in ((s2.at[:, chip], S_B), (s2.at[pl.ds(0, 2), chip], S_B), (yb.at[pl.ds(0, LAST)], S_P)):
+            remote(ref, ref, snd, R_B, peer).wait_send()
 
     @pl.when(core == 0)
     def _():
         tails()
         send_d[0].wait_send()
-        for n in range(NCH):
+        remote(pb, pb, S_P, R_B, peer).wait_send()
+        for n in range(LAST):
             send_y[n].wait_recv()
-            hb[:, :, at(n, CW)] = yb[n].astype(BF16).reshape(S, B, CW)
-
-    for ref, snd in ((mlall.at[pl.ds(0, 3)], S_ML), (obuf.at[1 - core], S_O), (c2.at[:, chip, pl.ds(0, 6)], S_C), (oall.at[core], S_G), (pb, S_P)):
+            put(n)
+        for c in send_last:
+            c.wait_recv()
+        finish(LAST)
+        put(LAST)
+
+    for ref, snd in ((mlall.at[pl.ds(0, 3)], S_ML), (obuf.at[1 - core], S_O), (c2.at[:, chip, pl.ds(0, 6)], S_C), (oall.at[core], S_G)):
         remote(ref, ref, snd, R_ML, partner).wait_send()
 
 

time: 22.4 us -> 21.8 us (0.973)
  Pallas kernels: 21.7 us -> 21.1 us
    pallas_call x1, Pallas kernels: 20.9 us -> 20.3 us  [layer_steps(): pl.pallas_call(kernel, out_shape=tuple((V(*o) for o in outs)), in_specs=[...]
where the time goes in v8:
time: 21.8 us; the launch traced here: 21.7 us
  Pallas kernels  21.1 us (97%)
  between operations  0.65 us (3%)
    pallas_call x1, Pallas kernels, layer_steps(): pl.pallas_call(kernel, out_shape=tuple((V(*o) for o in outs)), in_specs=[...  20.3 us
    pallas_call x1, Pallas kernels, layer_steps(): pl.pallas_call(write_kernel, out_shape=tuple((jax.ShapeDtypeStruct(*o) fo...  0.73 us

profile of v8, /device:TPU:0, one launch (start us, length us, event | category | flops | bytes accessed | tf_op | source)
XLA Modules:
  0.0 21.7 jit_solution(14379754571120365278)
XLA Ops:
  0.6 20.3 %shard_map.256 = (bf16[3,16,1024]{2,1,0:T(8,128)(2,1)S(1)}, bf16[16,3,8,64]{3,2,1,0:T(8,128)(2,1)S(1)}, bf16[16,3,8,64]{3,2,1,0:T(8,128)(2,1)S(1)}) custom-call(bf16[16,1024]{1,0:T(8,128)(2,1)} %x_first.1, bf16[2,16,1024]{2,1,0:T(8,128)(2,1)} %next_emb.1, bf16[16,8,64,256]{3,2,1,0:T(8,128)(2,1)} %bitcast.13, bf16[16,8,64,256]{3,2,1,0:T(8,128)(2,1)} %bitcast.14, ...), custom_call_target="tpu_custom_call" | custom-call | tf_op jit(solution)/shard_map/pallas_call | solution.py:557
  21.0 0.7 %shard_map.257 = (bf16[3,16,1024]{2,1,0:T(8,128)(2,1)}, bf16[16,3,8,64]{3,2,1,0:T(8,128)(2,1)}, bf16[16,3,8,64]{3,2,1,0:T(8,128)(2,1)}) custom-call(bf16[3,16,1024]{2,1,0:T(8,128)(2,1)S(1)} %get-tuple-element.6.h, bf16[16,3,8,64]{3,2,1,0:T(8,128)(2,1)S(1)} %get-tuple-element.7.tk, bf16[16,3,8,64]{3,2,1,0:T(8,128)(2,1)S(1)} %get-tuple-element.8.tv), custom_call_target="tpu_custom_call" | custom-call | tf_op jit(solution)/shard_map/pallas_call | solution.py:565

commit v9 on v8

--- a/solution.py
+++ b/solution.py
@@ -32,7 +32,7 @@
 
 GROUPS = 8
 SMALL, PARTS = 8, 4
-L_SMALL, L_WQ, L_K, L_V, L_WO, L_GU, L_DN, NLOCAL = itertools.accumulate((SMALL, 2, PARTS, PARTS, 1, PARTS, 2), initial=0)
+L_SMALL, L_WQ, L_K, L_V, L_WO, L_GU, L_DN, NLOCAL = itertools.accumulate((SMALL, 2, PARTS, PARTS, 1, PARTS, 3), initial=0)
 R_ML, R_O, R_C, R_G, R_P, R_B, NRECV = itertools.accumulate((3, 2, 2, 2, NCH, NCH + 1), initial=0)
 S_ML, S_O, S_C, S_G, S_P, S_B, NSEND = range(7)
 LN = 128
@@ -114,7 +114,7 @@
         return local(src.at[sl], dst.at[sl], sem)
 
     def down_copy(m, e, n):
-        sl = (pl.ds(e, n), pl.ds(0, FS), pl.ds(m * 2 * CW, 2 * CW))
+        sl = (pl.ds(e, n), pl.ds(0, FS), pl.ds(0, 2 * CW) if m == 0 else pl.ds((m + 1) * CW, CW))
         return local(wd_h.at[sl], wd.at[sl], L_DN + m)
 
     for c in first + cp_wq + cp_k[:3] + cp_v[:1] + cp_k[3:]:
@@ -246,7 +246,7 @@
     for i in FOUR:
         scores(own, 4 + i)
     cp_v[1].wait()
-    for m in TWO:
+    for m in range(3):
         for i in range(GROUPS):
             down_copy(m, i * 4, 4).start()
     for i in EIGHT:
@@ -444,8 +444,7 @@
             mix(i)
 
     for m in range(3):
-        if m < 2:
-            down_copy(m, 0, E).wait()
+        down_copy(m, 0, E).wait()
 
         @pl.when(here)
         def _():

time: 21.8 us -> 21.8 us (level)
  no operation moved by 1% of the time
where the time goes in v9:
time: 21.8 us; the launch traced here: 21.7 us
  Pallas kernels  21.1 us (97%)
  between operations  0.65 us (3%)
    pallas_call x1, Pallas kernels, layer_steps(): pl.pallas_call(kernel, out_shape=tuple((V(*o) for o in outs)), in_specs=[...  20.3 us
    pallas_call x1, Pallas kernels, layer_steps(): pl.pallas_call(write_kernel, out_shape=tuple((jax.ShapeDtypeStruct(*o) fo...  0.73 us

profile of v9, /device:TPU:0, one launch (start us, length us, event | category | flops | bytes accessed | tf_op | source)
XLA Modules:
  0.0 21.7 jit_solution(4117140050794102997)
XLA Ops:
  0.6 20.3 %shard_map.256 = (bf16[3,16,1024]{2,1,0:T(8,128)(2,1)S(1)}, bf16[16,3,8,64]{3,2,1,0:T(8,128)(2,1)S(1)}, bf16[16,3,8,64]{3,2,1,0:T(8,128)(2,1)S(1)}) custom-call(bf16[16,1024]{1,0:T(8,128)(2,1)} %x_first.1, bf16[2,16,1024]{2,1,0:T(8,128)(2,1)} %next_emb.1, bf16[16,8,64,256]{3,2,1,0:T(8,128)(2,1)} %bitcast.13, bf16[16,8,64,256]{3,2,1,0:T(8,128)(2,1)} %bitcast.14, ...), custom_call_target="tpu_custom_call" | custom-call | tf_op jit(solution)/shard_map/pallas_call | solution.py:556
  21.0 0.7 %shard_map.257 = (bf16[3,16,1024]{2,1,0:T(8,128)(2,1)}, bf16[16,3,8,64]{3,2,1,0:T(8,128)(2,1)}, bf16[16,3,8,64]{3,2,1,0:T(8,128)(2,1)}) custom-call(bf16[3,16,1024]{2,1,0:T(8,128)(2,1)S(1)} %get-tuple-element.6.h, bf16[16,3,8,64]{3,2,1,0:T(8,128)(2,1)S(1)} %get-tuple-element.7.tk, bf16[16,3,8,64]{3,2,1,0:T(8,128)(2,1)S(1)} %get-tuple-element.8.tv), custom_call_target="tpu_custom_call" | custom-call | tf_op jit(solution)/shard_map/pallas_call | solution.py:564

commit v10 on v9

--- a/solution.py
+++ b/solution.py
@@ -117,7 +117,7 @@
         sl = (pl.ds(e, n), pl.ds(0, FS), pl.ds(0, 2 * CW) if m == 0 else pl.ds((m + 1) * CW, CW))
         return local(wd_h.at[sl], wd.at[sl], L_DN + m)
 
-    for c in first + cp_wq + cp_k[:3] + cp_v[:1] + cp_k[3:]:
+    for c in cp_wq[:1] + first + cp_wq[1:] + cp_k[:3] + cp_v[:1] + cp_k[3:]:
         c.start()
     bar = pltpu.get_barrier_semaphore()
     for dev in (partner, peer, diag):

time: 21.8 us -> 21.9 us (level)
  no operation moved by 1% of the time
where the time goes in v10:
time: 21.9 us; the launch traced here: 21.8 us
  Pallas kernels  21.2 us (97%)
  between operations  0.65 us (3%)
    pallas_call x1, Pallas kernels, layer_steps(): pl.pallas_call(kernel, out_shape=tuple((V(*o) for o in outs)), in_specs=[...  20.4 us
    pallas_call x1, Pallas kernels, layer_steps(): pl.pallas_call(write_kernel, out_shape=tuple((jax.ShapeDtypeStruct(*o) fo...  0.73 us

profile of v10, /device:TPU:0, one launch (start us, length us, event | category | flops | bytes accessed | tf_op | source)
XLA Modules:
  0.0 21.8 jit_solution(1729450881193265210)
XLA Ops:
  0.6 20.4 %shard_map.256 = (bf16[3,16,1024]{2,1,0:T(8,128)(2,1)S(1)}, bf16[16,3,8,64]{3,2,1,0:T(8,128)(2,1)S(1)}, bf16[16,3,8,64]{3,2,1,0:T(8,128)(2,1)S(1)}) custom-call(bf16[16,1024]{1,0:T(8,128)(2,1)} %x_first.1, bf16[2,16,1024]{2,1,0:T(8,128)(2,1)} %next_emb.1, bf16[16,8,64,256]{3,2,1,0:T(8,128)(2,1)} %bitcast.13, bf16[16,8,64,256]{3,2,1,0:T(8,128)(2,1)} %bitcast.14, ...), custom_call_target="tpu_custom_call" | custom-call | tf_op jit(solution)/shard_map/pallas_call | solution.py:556
  21.1 0.7 %shard_map.257 = (bf16[3,16,1024]{2,1,0:T(8,128)(2,1)}, bf16[16,3,8,64]{3,2,1,0:T(8,128)(2,1)}, bf16[16,3,8,64]{3,2,1,0:T(8,128)(2,1)}) custom-call(bf16[3,16,1024]{2,1,0:T(8,128)(2,1)S(1)} %get-tuple-element.6.h, bf16[16,3,8,64]{3,2,1,0:T(8,128)(2,1)S(1)} %get-tuple-element.7.tk, bf16[16,3,8,64]{3,2,1,0:T(8,128)(2,1)S(1)} %get-tuple-element.8.tv), custom_call_target="tpu_custom_call" | custom-call | tf_op jit(solution)/shard_map/pallas_call | solution.py:564

commit v11 on v9

--- a/solution.py
+++ b/solution.py
@@ -32,7 +32,7 @@
 
 GROUPS = 8
 SMALL, PARTS = 8, 4
-L_SMALL, L_WQ, L_K, L_V, L_WO, L_GU, L_DN, NLOCAL = itertools.accumulate((SMALL, 2, PARTS, PARTS, 1, PARTS, 3), initial=0)
+L_SMALL, L_WQ, L_K, L_V, L_WO, L_GU, L_DN, NLOCAL = itertools.accumulate((SMALL, 2, PARTS, PARTS, 1, PARTS, NCH), initial=0)
 R_ML, R_O, R_C, R_G, R_P, R_B, NRECV = itertools.accumulate((3, 2, 2, 2, NCH, NCH + 1), initial=0)
 S_ML, S_O, S_C, S_G, S_P, S_B, NSEND = range(7)
 LN = 128
@@ -114,7 +114,7 @@
         return local(src.at[sl], dst.at[sl], sem)
 
     def down_copy(m, e, n):
-        sl = (pl.ds(e, n), pl.ds(0, FS), pl.ds(0, 2 * CW) if m == 0 else pl.ds((m + 1) * CW, CW))
+        sl = (pl.ds(e, n), pl.ds(0, FS), pl.ds(m * CW, CW))
         return local(wd_h.at[sl], wd.at[sl], L_DN + m)
 
     for c in first + cp_wq + cp_k[:3] + cp_v[:1] + cp_k[3:]:
@@ -246,7 +246,7 @@
     for i in FOUR:
         scores(own, 4 + i)
     cp_v[1].wait()
-    for m in range(3):
+    for m in range(NCH):
         for i in range(GROUPS):
             down_copy(m, i * 4, 4).start()
     for i in EIGHT:
@@ -443,25 +443,20 @@
         for i in range(3, 7):
             mix(i)
 
-    for m in range(3):
+    for m in range(NCH):
         down_copy(m, 0, E).wait()
 
         @pl.when(here)
         def _():
             if m == 0:
                 mix(7)
-                part = rounded(down(0, 0, E, 2 * CW))
-                pb[0] = part[:, :CW]
-                pb[1] = part[:, CW:]
-            else:
-                for h in TWO:
-                    dsum[h] = down(m + 1, h * (E // 2), E // 2, CW)
-                pb[m + 1] = rounded(dsum[0] + dsum[1])
+            for h in TWO:
+                dsum[h] = down(m, h * (E // 2), E // 2, CW)
+            pb[m] = rounded(dsum[0] + dsum[1])
 
         @pl.when(core == 0)
         def _():
-            for n in ((0, 1) if m == 0 else (m + 1,)):
-                send_a[n].start()
+            send_a[m].start()
             if m == 0:
                 send_d[0].start()
 
@@ -469,7 +464,7 @@
         def _():
             if m == 0:
                 send_d[1].start()
-            for n in ((), (0, 1), (2, LAST))[m]:
+            for n in ((), (), (0, 1), (2, LAST))[m]:
                 send_a[n].wait_recv()
                 s2[n, chip] = ab[n] + pb[n]
                 if n == LAST:

time: 21.8 us -> 21.8 us (level)
  no operation moved by 1% of the time
where the time goes in v11:
time: 21.8 us; the launch traced here: 21.7 us
  Pallas kernels  21 us (96%)
  between operations  0.65 us (3%)
    pallas_call x1, Pallas kernels, layer_steps(): pl.pallas_call(kernel, out_shape=tuple((V(*o) for o in outs)), in_specs=[...  20.3 us
    pallas_call x1, Pallas kernels, layer_steps(): pl.pallas_call(write_kernel, out_shape=tuple((jax.ShapeDtypeStruct(*o) fo...  0.73 us

profile of v11, /device:TPU:0, one launch (start us, length us, event | category | flops | bytes accessed | tf_op | source)
XLA Modules:
  0.0 21.7 jit_solution(2218703396007382354)
XLA Ops:
  0.6 20.3 %shard_map.256 = (bf16[3,16,1024]{2,1,0:T(8,128)(2,1)S(1)}, bf16[16,3,8,64]{3,2,1,0:T(8,128)(2,1)S(1)}, bf16[16,3,8,64]{3,2,1,0:T(8,128)(2,1)S(1)}) custom-call(bf16[16,1024]{1,0:T(8,128)(2,1)} %x_first.1, bf16[2,16,1024]{2,1,0:T(8,128)(2,1)} %next_emb.1, bf16[16,8,64,256]{3,2,1,0:T(8,128)(2,1)} %bitcast.13, bf16[16,8,64,256]{3,2,1,0:T(8,128)(2,1)} %bitcast.14, ...), custom_call_target="tpu_custom_call" | custom-call | tf_op jit(solution)/shard_map/pallas_call | solution.py:551
  20.9 0.7 %shard_map.257 = (bf16[3,16,1024]{2,1,0:T(8,128)(2,1)}, bf16[16,3,8,64]{3,2,1,0:T(8,128)(2,1)}, bf16[16,3,8,64]{3,2,1,0:T(8,128)(2,1)}) custom-call(bf16[3,16,1024]{2,1,0:T(8,128)(2,1)S(1)} %get-tuple-element.6.h, bf16[16,3,8,64]{3,2,1,0:T(8,128)(2,1)S(1)} %get-tuple-element.7.tk, bf16[16,3,8,64]{3,2,1,0:T(8,128)(2,1)S(1)} %get-tuple-element.8.tv), custom_call_target="tpu_custom_call" | custom-call | tf_op jit(solution)/shard_map/pallas_call | solution.py:559

commit v12 on v11

--- a/solution.py
+++ b/solution.py
@@ -501,12 +501,13 @@
         send_d[0].wait_send()
         remote(pb, pb, S_P, R_B, peer).wait_send()
         for n in range(LAST):
+            if n == LAST - 1:
+                for c in send_last:
+                    c.wait_recv()
+                finish(LAST)
+                put(LAST)
             send_y[n].wait_recv()
             put(n)
-        for c in send_last:
-            c.wait_recv()
-        finish(LAST)
-        put(LAST)
 
     for ref, snd in ((mlall.at[pl.ds(0, 3)], S_ML), (obuf.at[1 - core], S_O), (c2.at[:, chip, pl.ds(0, 6)], S_C), (oall.at[core], S_G)):
         remote(ref, ref, snd, R_ML, partner).wait_send()

time: 21.8 us -> 21.7 us (level)
  no operation moved by 1% of the time
where the time goes in v12:
time: 21.7 us
  Pallas kernels  21 us (97%)
  between operations  0.65 us (3%)
    pallas_call x1, Pallas kernels, layer_steps(): pl.pallas_call(kernel, out_shape=tuple((V(*o) for o in outs)), in_specs=[...  20.3 us
    pallas_call x1, Pallas kernels, layer_steps(): pl.pallas_call(write_kernel, out_shape=tuple((jax.ShapeDtypeStruct(*o) fo...  0.73 us

profile of v12, /device:TPU:0, one launch (start us, length us, event | category | flops | bytes accessed | tf_op | source)
XLA Modules:
  0.0 21.7 jit_solution(3346477082624677807)
XLA Ops:
  0.6 20.3 %shard_map.256 = (bf16[3,16,1024]{2,1,0:T(8,128)(2,1)S(1)}, bf16[16,3,8,64]{3,2,1,0:T(8,128)(2,1)S(1)}, bf16[16,3,8,64]{3,2,1,0:T(8,128)(2,1)S(1)}) custom-call(bf16[16,1024]{1,0:T(8,128)(2,1)} %x_first.1, bf16[2,16,1024]{2,1,0:T(8,128)(2,1)} %next_emb.1, bf16[16,8,64,256]{3,2,1,0:T(8,128)(2,1)} %bitcast.13, bf16[16,8,64,256]{3,2,1,0:T(8,128)(2,1)} %bitcast.14, ...), custom_call_target="tpu_custom_call" | custom-call | tf_op jit(solution)/shard_map/pallas_call | solution.py:552
  20.9 0.7 %shard_map.257 = (bf16[3,16,1024]{2,1,0:T(8,128)(2,1)}, bf16[16,3,8,64]{3,2,1,0:T(8,128)(2,1)}, bf16[16,3,8,64]{3,2,1,0:T(8,128)(2,1)}) custom-call(bf16[3,16,1024]{2,1,0:T(8,128)(2,1)S(1)} %get-tuple-element.6.h, bf16[16,3,8,64]{3,2,1,0:T(8,128)(2,1)S(1)} %get-tuple-element.7.tk, bf16[16,3,8,64]{3,2,1,0:T(8,128)(2,1)S(1)} %get-tuple-element.8.tv), custom_call_target="tpu_custom_call" | custom-call | tf_op jit(solution)/shard_map/pallas_call | solution.py:560
